TPU v7x, 32 devices: a whole 2x2x4 slice. The times are simulated.
32 devices in a mesh: gp: 32 (over z, y, x, core).
Axes of the slice: x: 2, y: 2, z: 4, core: 2. Of those that a mesh axis runs over, the one named last changes fastest.
Arguments:
- features: bfloat16 [65536, 128], P('gp')
- labels: int32 [65536], P('gp')
- train_mask: float32 [65536], P('gp')
- send_idx: int32 [1024, 512], P('gp')
- src_idx: int32 [196608], P('gp')
- dst_idx: int32 [196608], P('gp')
- inv_deg: float32 [65536], P('gp')
- w_self_1: bfloat16 [128, 256], replicated
- w_neigh_1: bfloat16 [128, 256], replicated
- bias_1: float32 [256], replicated
- w_self_2: bfloat16 [256, 256], replicated
- w_neigh_2: bfloat16 [256, 256], replicated
- bias_2: float32 [256], replicated
- w_self_3: bfloat16 [256, 40], replicated
- w_neigh_3: bfloat16 [256, 40], replicated
- bias_3: float32 [40], replicated
Outputs:
- output 1: float32 [], replicated
- output 2: float32 [128, 256], replicated
- output 3: float32 [128, 256], replicated
- output 4: float32 [256], replicated
- output 5: float32 [256, 256], replicated
- output 6: float32 [256, 256], replicated
- output 7: float32 [256], replicated
- output 8: float32 [256, 40], replicated
- output 9: float32 [256, 40], replicated
- output 10: float32 [40], replicated
All inputs are finite; a program needn't handle non-finite values.
Results may differ from a plain program's by a relative error of at most 0.0106418.
Values are sent between devices in bfloat16 or wider.
A program may use at most 1 GiB of HBM per device.

v0:
```python
import jax
import jax.numpy as jnp
from jax import lax
from jax.sharding import PartitionSpec as P

GROUP_AXIS = 'gp'


def aggregate(table, src_idx, dst_idx, inv_deg):
    gathered = jnp.take(table, src_idx, axis=0).astype(jnp.float32)
    summed = jax.ops.segment_sum(gathered, dst_idx, num_segments=inv_deg.shape[0], indices_are_sorted=True)
    return (summed * inv_deg[:, None]).astype(jnp.bfloat16)


def aggregate_grad(d_mean, src_idx, dst_idx, inv_deg, table_rows):
    d_sum = d_mean * inv_deg[:, None]
    return jax.ops.segment_sum(jnp.take(d_sum, dst_idx, axis=0), src_idx, num_segments=table_rows)


def weight_grads(h_in, neigh_mean, d_pre, d_pre_bf):
    g_self = jnp.einsum('nd,ne->de', h_in, d_pre_bf, preferred_element_type=jnp.float32)
    g_neigh = jnp.einsum('nd,ne->de', neigh_mean, d_pre_bf, preferred_element_type=jnp.float32)
    return g_self, g_neigh, jnp.sum(d_pre, axis=0)


def input_grads(d_pre_bf, w_self, w_neigh):
    d_self = jnp.einsum('ne,de->nd', d_pre_bf, w_self, preferred_element_type=jnp.float32)
    d_mean = jnp.einsum('ne,de->nd', d_pre_bf, w_neigh, preferred_element_type=jnp.float32)
    return d_self, d_mean


def head_grad(logits, labels, train_mask):
    log_prob = jax.nn.log_softmax(logits, axis=-1)
    is_label = labels[:, None] == jnp.arange(logits.shape[1], dtype=jnp.int32)[None, :]
    picked = jnp.sum(jnp.where(is_label, log_prob, 0.0), axis=-1)
    d_logits = (jnp.exp(log_prob) - is_label.astype(jnp.float32)) * train_mask[:, None]
    return jnp.sum(train_mask * -picked), d_logits


def solution(mesh):
    def device_step(features, labels, train_mask, send_idx, src_idx, dst_idx, inv_deg,
                    w_self_1, w_neigh_1, bias_1, w_self_2, w_neigh_2, bias_2,
                    w_self_3, w_neigh_3, bias_3):
        n_own = features.shape[0]
        send_flat = send_idx.reshape(-1)
        table_rows = n_own + send_flat.shape[0]

        def layer(hidden, w_self, w_neigh, bias):
            outgoing = jnp.take(hidden, send_flat, axis=0)
            received = lax.all_to_all(outgoing, GROUP_AXIS, 0, 0, tiled=True)
            table = jnp.concatenate([hidden, received], axis=0)
            neigh_mean = aggregate(table, src_idx, dst_idx, inv_deg)
            pre_act = (jnp.dot(hidden, w_self, preferred_element_type=jnp.float32)
                       + jnp.dot(neigh_mean, w_neigh, preferred_element_type=jnp.float32) + bias)
            return neigh_mean, pre_act

        def back_to_owners(d_mean):
            d_table = aggregate_grad(d_mean, src_idx, dst_idx, inv_deg, table_rows)
            returned = lax.all_to_all(d_table[n_own:].astype(jnp.bfloat16), GROUP_AXIS, 0, 0, tiled=True)
            owner_sum = jax.ops.segment_sum(returned.astype(jnp.float32), send_flat, num_segments=n_own)
            return d_table[:n_own] + owner_sum

        mean_1, pre_1 = layer(features, w_self_1, w_neigh_1, bias_1)
        hidden_1 = jax.nn.relu(pre_1).astype(jnp.bfloat16)
        mean_2, pre_2 = layer(hidden_1, w_self_2, w_neigh_2, bias_2)
        hidden_2 = jax.nn.relu(pre_2).astype(jnp.bfloat16)
        mean_3, logits = layer(hidden_2, w_self_3, w_neigh_3, bias_3)
        loss_sum, d_logits = head_grad(logits, labels, train_mask)
        totals = lax.psum(jnp.stack([loss_sum, jnp.sum(train_mask)]), GROUP_AXIS)

        d_pre_3 = d_logits / totals[1]
        d_bf_3 = d_pre_3.astype(jnp.bfloat16)
        g_self_3, g_neigh_3, g_bias_3 = weight_grads(hidden_2, mean_3, d_pre_3, d_bf_3)
        d_self_3, d_mean_3 = input_grads(d_bf_3, w_self_3, w_neigh_3)
        d_pre_2 = jnp.where(pre_2 > 0, d_self_3 + back_to_owners(d_mean_3), 0.0)
        d_bf_2 = d_pre_2.astype(jnp.bfloat16)
        g_self_2, g_neigh_2, g_bias_2 = weight_grads(hidden_1, mean_2, d_pre_2, d_bf_2)
        d_self_2, d_mean_2 = input_grads(d_bf_2, w_self_2, w_neigh_2)
        d_pre_1 = jnp.where(pre_1 > 0, d_self_2 + back_to_owners(d_mean_2), 0.0)
        d_bf_1 = d_pre_1.astype(jnp.bfloat16)
        g_self_1, g_neigh_1, g_bias_1 = weight_grads(features, mean_1, d_pre_1, d_bf_1)

        grads = lax.psum((g_self_1, g_neigh_1, g_bias_1, g_self_2, g_neigh_2, g_bias_2,
                          g_self_3, g_neigh_3, g_bias_3), GROUP_AXIS)
        return (totals[0] / totals[1],) + tuple(grads)

    sharded = P(GROUP_AXIS)
    whole = P()
    return jax.shard_map(device_step, mesh=mesh,
                         in_specs=(sharded,) * 7 + (whole,) * 9,
                         out_specs=(whole,) * 10, check_vma=False)
```

profile of v0, /device:TPU:0, one launch (start us, length us, event | category | flops | bytes accessed | tf_op | source)
XLA Modules:
  0.0 2044.5 jit_solution(6214998786076558714)
XLA Ops:
  7.2 0.9 compare_and_fusion.1
  8.1 0.9 copy.27
  9.1 56.0 %gather_fusion = bf16[16384,128]{1,0:T(8,128)(2,1)} fusion(bf16[2048,128]{1,0:T(8,128)(2,1)} %param.22, s32[16384]{0:T(1024)S(1)} %broadcast_clamp_fusion), kind=kCustom, calls=%fused_computation.6 | custom fusion | bytes 8454144 | tf_op jit(solution)/shard_map/jit(_take)/gather | solution.py:49
  65.1 7.6 broadcast_select_fusion.2
  72.8 7.5 all-to-all-start
  80.4 1.7 fusion.54
  82.2 90.3 %all-to-all-done = bf16[32,512,128]{2,1,0:T(8,128)(2,1)} async-done(((bf16[32,512,128]{2,1,0:T(8,128)(2,1)}), bf16[32,512,128]{2,1,0:T(8,128)(2,1)}, u32[]{:S(2)}, u32[]{:S(2)}) %all-to-all-start) | async-done | bytes 4194336 | tf_op jit(solution)/shard_map/all_to_all | solution.py:50
  172.5 6.4 pad_maximum_fusion.2
  178.9 74.7 %scatter_custom_fusion = f32[2048,128]{1,0:T(8,128)S(1)} fusion(s32[6144]{0:T(1024)S(1)} %copy-done.13, pred[6144]{0:T(1024)(128)(4,1)S(1)} %compare_and_fusion.3, bf16[]{:T(256)} %constant.63.clone.1, f32[]{:T(128)} %constant.54.clone.1, bf16[18432,128]{1,0:T(8,128)(2,1)} %pad_maximum_fusion.2, s32[6144]{0:T(1024)S(1)} %fusion.40), kind=kCustom, calls=%fused_computation.41 | custom fusion | flops 2359296 | bytes 5797894 | tf_op jit(solution)/shard_map/scatter-add | solution.py:11
  253.6 3.8 maximum_convert_fusion.1
  257.4 64.8 %gather_fusion.1 = bf16[16384,256]{1,0:T(8,128)(2,1)} fusion(bf16[2048,256]{1,0:T(8,128)(2,1)S(1)} %get-tuple-element.38, s32[16384]{0:T(1024)S(1)} %fusion.39), kind=kCustom, calls=%fused_computation.clone | custom fusion | bytes 16842752 | tf_op jit(solution)/shard_map/jit(_take)/gather | solution.py:49
  322.3 8.0 broadcast_select_fusion.1
  330.3 6.5 all-to-all-start.1
  336.8 1.8 fusion.55
  338.6 173.4 %all-to-all-done.1 = bf16[32,512,256]{2,1,0:T(8,128)(2,1)} async-done(((bf16[32,512,256]{2,1,0:T(8,128)(2,1)}), bf16[32,512,256]{2,1,0:T(8,128)(2,1)}, u32[]{:S(2)}, u32[]{:S(2)}) %all-to-all-start.1) | async-done | bytes 8388640 | tf_op jit(solution)/shard_map/all_to_all | solution.py:50
  512.1 13.2 pad_maximum_fusion
  525.2 77.0 %scatter_custom_fusion.1 = f32[2048,256]{1,0:T(8,128)} fusion(s32[6144]{0:T(1024)S(1)} %copy-done.13, pred[6144]{0:T(1024)(128)(4,1)S(1)} %compare_and_fusion.3, bf16[]{:T(256)} %constant.63.clone.1, f32[]{:T(128)} %constant.54.clone.1, bf16[18432,256]{1,0:T(8,128)(2,1)} %pad_maximum_fusion, s32[6144]{0:T(1024)S(1)} %fusion.40), kind=kCustom, calls=%fused_computation.33 | custom fusion | flops 4718592 | bytes 11565062 | tf_op jit(solution)/shard_map/scatter-add | solution.py:11
  602.2 4.1 maximum_convert_fusion
  606.4 64.8 %gather_fusion.2 = bf16[16384,256]{1,0:T(8,128)(2,1)} fusion(bf16[2048,256]{1,0:T(8,128)(2,1)S(1)} %get-tuple-element.40, s32[16384]{0:T(1024)S(1)} %fusion.39), kind=kCustom, calls=%fused_computation.3.clone | custom fusion | bytes 16842752 | tf_op jit(solution)/shard_map/jit(_take)/gather | solution.py:49
  671.2 8.0 broadcast_select_fusion
  679.2 12.7 all-to-all-start.2
  692.4 174.8 %all-to-all-done.2 = bf16[32,512,256]{2,1,0:T(8,128)(2,1)} async-done(((bf16[32,512,256]{2,1,0:T(8,128)(2,1)}), bf16[32,512,256]{2,1,0:T(8,128)(2,1)}, u32[]{:S(2)}, u32[]{:S(2)}) %all-to-all-start.2) | async-done | bytes 8388640 | tf_op jit(solution)/shard_map/all_to_all | solution.py:50
  867.2 13.2 pad_maximum_fusion.1
  880.3 76.9 %scatter_custom_fusion.2 = f32[2048,256]{1,0:T(8,128)} fusion(s32[6144]{0:T(1024)S(1)} %copy-done.13, pred[6144]{0:T(1024)(128)(4,1)S(1)} %compare_and_fusion.3, bf16[]{:T(256)} %constant.63.clone.1, f32[]{:T(128)} %constant.54.clone.1, bf16[18432,256]{1,0:T(8,128)(2,1)} %pad_maximum_fusion.1, s32[6144]{0:T(1024)S(1)} %fusion.40), kind=kCustom, calls=%fused_computation.31 | custom fusion | flops 4718592 | bytes 11565062 | tf_op jit(solution)/shard_map/scatter-add | solution.py:11
  957.3 2.1 fusion.53
  960.2 1.4 pad_maximum_fusion.3
  961.6 46.7 %psum.70 = f32[2]{0:T(128)S(1)} all-reduce(f32[2]{0:T(128)S(1)} %pad_maximum_fusion.3), channel_id=1, replica_groups=mesh['gp'=32] {'gp'}, use_global_device_ids=true, to_apply=%region_8.11 | all-reduce | flops 2 | bytes 16 | tf_op jit(solution)/shard_map/psum | solution.py:69
  1008.8 1.5 fusion.42
  1010.3 2.5 convolution_multiply_fusion
  1012.8 78.0 %scatter_custom_fusion.3 = f32[18432,256]{1,0:T(8,128)} fusion(s32[6144]{0:T(1024)} %param.26, f32[]{:T(128)} %constant.54.clone.1, f32[]{:T(128)} %constant.47.clone.2, pred[6144]{0:T(1024)(128)(4,1)S(1)} %compare_and_fusion.2, f32[2048,256]{1,0:T(8,128)} %convolution_multiply_fusion, s32[6144]{0:T(1024)S(1)} %fusion.41), kind=kCustom, calls=%fused_computation.25 | custom fusion | flops 3145728 | bytes 21003264 | tf_op jit(solution)/shard_map/scatter-add | solution.py:17
  1090.8 8.9 slice.72
  1099.7 5.4 all-to-all-start.3
  1105.1 3.4 convolution_add_fusion
  1108.4 172.8 %all-to-all-done.3 = bf16[32,512,256]{2,1,0:T(8,128)(2,1)} async-done(((bf16[32,512,256]{2,1,0:T(8,128)(2,1)}), bf16[32,512,256]{2,1,0:T(8,128)(2,1)}, u32[]{:S(2)}, u32[]{:S(2)}) %all-to-all-start.3) | async-done | bytes 8388640 | tf_op jit(solution)/shard_map/all_to_all | solution.py:59
  1281.2 92.2 %scatter_custom_fusion.4 = f32[2048,256]{1,0:T(8,128)} fusion(f32[2048,256]{1,0:T(8,128)} %convolution_add_fusion, s32[16384]{0:T(1024)S(1)} %bitcast.60, bf16[16384,256]{1,0:T(8,128)(2,1)} %bitcast.16), kind=kCustom, calls=%fused_computation.19 | custom fusion | flops 8388608 | bytes 10485760 | tf_op jit(solution)/shard_map/scatter-add | solution.py:60
  1373.4 2.5 fusion.36
  1376.0 1.0 copy-done.2
  1377.0 1.8 convolution_multiply_fusion.1
  1378.8 78.0 %scatter_custom_fusion.5 = f32[18432,256]{1,0:T(8,128)} fusion(s32[6144]{0:T(1024)} %param.26, f32[]{:T(128)} %constant.54.clone.1, f32[]{:T(128)} %constant.47.clone.2, pred[6144]{0:T(1024)(128)(4,1)S(1)} %compare_and_fusion.2, f32[2048,256]{1,0:T(8,128)} %convolution_multiply_fusion.1, s32[6144]{0:T(1024)S(1)} %fusion.41), kind=kCustom, calls=%fused_computation.23 | custom fusion | flops 3145728 | bytes 21003264 | tf_op jit(solution)/shard_map/scatter-add | solution.py:17
  1456.8 8.9 slice.71
  1465.7 11.7 all-to-all-start.4
  1477.4 0.9 fusion.58
  1478.3 2.7 fusion.51
  1481.1 2.4 fusion.57
  1483.5 1.6 fusion.50
  1485.0 2.1 convolution_add_fusion.1
  1487.1 166.4 %all-to-all-done.4 = bf16[32,512,256]{2,1,0:T(8,128)(2,1)} async-done(((bf16[32,512,256]{2,1,0:T(8,128)(2,1)}), bf16[32,512,256]{2,1,0:T(8,128)(2,1)}, u32[]{:S(2)}, u32[]{:S(2)}) %all-to-all-start.4) | async-done | bytes 8388640 | tf_op jit(solution)/shard_map/all_to_all | solution.py:59
  1653.5 90.2 %scatter_custom_fusion.6 = f32[2048,256]{1,0:T(8,128)S(1)} fusion(f32[2048,256]{1,0:T(8,128)S(1)} %convolution_add_fusion.1, s32[16384]{0:T(1024)S(1)} %bitcast.61, bf16[16384,256]{1,0:T(8,128)(2,1)} %bitcast.17), kind=kCustom, calls=%fused_computation.17 | custom fusion | flops 8388608 | bytes 10485760 | tf_op jit(solution)/shard_map/scatter-add | solution.py:60
  1743.7 1.3 copy-done.5
  1745.1 2.7 fusion.34
  1747.8 1.4 fusion.49
  1749.1 1.1 convolution_bitcast_fusion
  1750.4 3.9 fusion.33
  1755.6 132.6 %all-reduce.7.cloned.1.call-done = (f32[128,256]{0,1:T(8,128)}, f32[128,256]{1,0:T(8,128)}, f32[256,256]{1,0:T(8,128)}, f32[256,256]{1,0:T(8,128)}) async-done(((f32[128,256]{0,1:T(8,128)}, f32[128,256]{1,0:T(8,128)}, f32[256,256]{1,0:T(8,128)}, f32[256,256]{1,0:T(8,128)}), (f32[128,256]{0,1:T(8,128)}, f32[128,256]{1,0:T(8,128)}, f32[256,256]{1,0:T(8,128)}, ...) | async-done | bytes 786448 | tf_op jit(solution)/shard_map/psum | solution.py:83
  1888.3 1.7 copy.26
  1889.9 134.8 %all-reduce.5.cloned.1.call-done = (f32[256]{0:T(256)}, f32[256]{0:T(256)}, f32[256,40]{0,1:T(8,128)}, f32[256,40]{0,1:T(8,128)}, f32[40]{0:T(128)}) async-done(((f32[256]{0:T(256)}, f32[256]{0:T(256)}, f32[256,40]{0,1:T(8,128)}, f32[256,40]{0,1:T(8,128)}, f32[40]{0:T(128)}), (f32[256]{0:T(256)}, f32[256]{0:T(256)}, f32[256,40]{0,1:T(8,128)}, f32[256,40]{0,1:T(8,128)}, ...) | async-done | bytes 84144 | tf_op jit(solution)/shard_map/psum | solution.py:83
  2024.8 1.6 copy.40
  2026.3 1.2 copy.41
  2027.6 1.7 copy.42
  2029.2 1.7 copy.43
  2030.9 1.2 copy.44
  2032.1 1.4 copy.45
  2033.5 1.4 copy.46
  2034.9 1.1 copy.47
  (63 shorter events, 2.1 us)
Async XLA Ops:
  7.2 595.1 %copy-start = (bf16[256,256]{1,0:T(8,128)(2,1)S(1)}, bf16[256,256]{1,0:T(8,128)(2,1)}, u32[]{:S(2)}) copy-start(bf16[256,256]{1,0:T(8,128)(2,1)} %param.33) | copy-start | bytes 393220
  72.8 7.5 copy-start.9
  72.8 7.6 copy-start.14
  72.8 7.6 copy-start.1
  72.8 7.6 copy-start.18
  72.8 99.7 %all-to-all-start = ((bf16[32,512,128]{2,1,0:T(8,128)(2,1)}), bf16[32,512,128]{2,1,0:T(8,128)(2,1)}, u32[]{:S(2)}, u32[]{:S(2)}) async-start(bf16[32,512,128]{2,1,0:T(8,128)(2,1)} %broadcast_select_fusion.2), calls=%async_computation | async-start | bytes 8388608 | tf_op jit(solution)/shard_map/all_to_all | solution.py:50
  172.5 6.4 copy-start.13
  178.9 74.7 %copy-start.10 = (f32[2048]{0:T(1024)S(1)}, f32[2048]{0:T(1024)}, u32[]{:S(2)}) copy-start(f32[2048]{0:T(1024)} %param.28) | copy-start | bytes 24580
  178.9 74.7 %copy-start.17 = (bf16[128,256]{1,0:T(8,128)(2,1)S(1)}, bf16[128,256]{1,0:T(8,128)(2,1)}, u32[]{:S(2)}) copy-start(bf16[128,256]{1,0:T(8,128)(2,1)} %param.30) | copy-start | bytes 196612
  178.9 74.7 %copy-start.22 = (f32[256]{0:T(256)S(1)}, f32[256]{0:T(256)}, u32[]{:S(2)}) copy-start(f32[256]{0:T(256)} %param.31) | copy-start | bytes 3076
  253.6 68.6 %copy-start.7 = (f32[2048,128]{1,0:T(8,128)}, f32[2048,128]{1,0:T(8,128)S(1)}, u32[]{:S(2)}) copy-start(f32[2048,128]{1,0:T(8,128)S(1)} %scatter_custom_fusion) | copy-start | bytes 3145732
  330.3 6.6 copy-start.11
  330.3 181.8 %all-to-all-start.1 = ((bf16[32,512,256]{2,1,0:T(8,128)(2,1)}), bf16[32,512,256]{2,1,0:T(8,128)(2,1)}, u32[]{:S(2)}, u32[]{:S(2)}) async-start(bf16[32,512,256]{2,1,0:T(8,128)(2,1)} %bitcast.52), calls=%async_computation.1 | async-start | bytes 16777216 | tf_op jit(solution)/shard_map/all_to_all | solution.py:50
  525.2 77.0 %copy-start.21 = (f32[256]{0:T(256)S(1)}, f32[256]{0:T(256)}, u32[]{:S(2)}) copy-start(f32[256]{0:T(256)} %param.34) | copy-start | bytes 3076
  679.2 12.7 copy-start.15
  679.2 187.9 %all-to-all-start.2 = ((bf16[32,512,256]{2,1,0:T(8,128)(2,1)}), bf16[32,512,256]{2,1,0:T(8,128)(2,1)}, u32[]{:S(2)}, u32[]{:S(2)}) async-start(bf16[32,512,256]{2,1,0:T(8,128)(2,1)} %bitcast.51), calls=%async_computation.2 | async-start | bytes 16777216 | tf_op jit(solution)/shard_map/all_to_all | solution.py:50
  880.3 79.2 %copy-start.19 = (s32[2048]{0:T(1024)S(1)}, s32[2048]{0:T(1024)}, u32[]{:S(2)}) copy-start(s32[2048]{0:T(1024)} %param.23) | copy-start | bytes 24580
  880.3 79.2 %copy-start.20 = (f32[2048]{0:T(1024)S(1)}, f32[2048]{0:T(1024)}, u32[]{:S(2)}) copy-start(f32[2048]{0:T(1024)} %param.24) | copy-start | bytes 24580
  1099.7 5.4 copy-start.16
  1099.7 181.5 %all-to-all-start.3 = ((bf16[32,512,256]{2,1,0:T(8,128)(2,1)}), bf16[32,512,256]{2,1,0:T(8,128)(2,1)}, u32[]{:S(2)}, u32[]{:S(2)}) async-start(bf16[32,512,256]{2,1,0:T(8,128)(2,1)} %bitcast.54), calls=%async_computation.3 | async-start | bytes 16777216 | tf_op jit(solution)/shard_map/all_to_all | solution.py:59
  1376.0 1.0 copy-start.2
  1465.7 187.8 %all-to-all-start.4 = ((bf16[32,512,256]{2,1,0:T(8,128)(2,1)}), bf16[32,512,256]{2,1,0:T(8,128)(2,1)}, u32[]{:S(2)}, u32[]{:S(2)}) async-start(bf16[32,512,256]{2,1,0:T(8,128)(2,1)} %bitcast.53), calls=%async_computation.4 | async-start | bytes 16777216 | tf_op jit(solution)/shard_map/all_to_all | solution.py:59
  1477.4 410.9 %all-reduce.7.cloned.1.call-start = ((), (), s32[]{:S(2)}) async-start(), calls=%async_computation.6 | async-start | bytes 1572864 | tf_op jit(solution)/shard_map/psum | solution.py:83
  1477.4 6.1 copy-start.3
  1477.4 6.0 copy-start.6
  1478.3 6.7 copy-start.12
  1743.7 1.4 copy-start.5
  1745.1 2.7 copy-start.8
  1745.1 5.3 copy-start.4
  1750.3 274.5 %all-reduce.5.cloned.1.call-start = ((), (), s32[]{:S(2)}) async-start(), calls=%async_computation.5 | async-start | bytes 168960 | tf_op jit(solution)/shard_map/psum | solution.py:83
Sparse Core Ops, SparseCore 0:
  1750.4 137.8 all-reduce.6
  1895.9 128.8 all-reduce.4
where the time goes:
time: 2050 us; the launch traced here: 2040 us
  waiting for transfers between devices  1050 us (51%)
  other arithmetic  637 us (31%)
  local copies, waits for them, and re-layouts  220 us (11%)
  blocking collectives  46.7 us (2%)
  starting transfers between devices  43.8 us (2%)
  matrix products  33.8 us (2%)
    all_to_all x3, waiting for transfers between devices, layer(): received = lax.all_to_all(outgoing, GROUP_AXIS, 0, 0, tiled=True)  439 us
    all_to_all x2, waiting for transfers between devices, back_to_owners(): lax.all_to_all(d_table[n_own:].astype(jnp.bfloat16), GROUP_AXIS, 0, 0, ti...  339 us
    psum x2, waiting for transfers between devices, device_step(): lax.psum((g_self_1, g_neigh_1, g_bias_1, g_self_2, g_neigh_2, g_bias_2, g...  267 us
    scatter-add x3, other arithmetic, aggregate(): jax.ops.segment_sum(gathered, dst_idx, num_segments=inv_deg.shape[0], ind...  229 us
    gather x3, local copies, waits for them, and re-layouts, layer(): outgoing = jnp.take(hidden, send_flat, axis=0)  186 us
    scatter-add x2, other arithmetic, back_to_owners(): jax.ops.segment_sum(returned.astype(jnp.float32), send_flat, num_segments...  182 us
    scatter-add x2, other arithmetic, aggregate_grad(): jax.ops.segment_sum(jnp.take(d_sum, dst_idx, axis=0), src_idx, num_segmen...  156 us
    psum x1, blocking collectives, device_step(): totals = lax.psum(jnp.stack([loss_sum, jnp.sum(train_mask)]), GROUP_AXIS)  46.7 us
  transfers between devices with their start and end apart: 7, of which 7 were waited for; matrix products, arithmetic and copies ran while one was open for 1% of the time, Pallas kernels for 0%

commit v1 on v0

--- a/solution.py
+++ b/solution.py
@@ -1,20 +1,215 @@
+import functools
+
 import jax
 import jax.numpy as jnp
 from jax import lax
+from jax.experimental import pallas as pl
+from jax.experimental.pallas import tpu as pltpu
 from jax.sharding import PartitionSpec as P
 
 GROUP_AXIS = 'gp'
-
-
-def aggregate(table, src_idx, dst_idx, inv_deg):
-    gathered = jnp.take(table, src_idx, axis=0).astype(jnp.float32)
-    summed = jax.ops.segment_sum(gathered, dst_idx, num_segments=inv_deg.shape[0], indices_are_sorted=True)
-    return (summed * inv_deg[:, None]).astype(jnp.bfloat16)
-
-
-def aggregate_grad(d_mean, src_idx, dst_idx, inv_deg, table_rows):
-    d_sum = d_mean * inv_deg[:, None]
-    return jax.ops.segment_sum(jnp.take(d_sum, dst_idx, axis=0), src_idx, num_segments=table_rows)
+LANES = 128
+DST_TILE = 256
+CHUNK = 256
+COLS = 512
+BATCH = 8
+VMEM_BYTES = 60 * 1024 * 1024
+F32 = jnp.float32
+BF16 = jnp.bfloat16
+
+
+def as_columns(row):
+    return jnp.broadcast_to(row, (LANES, LANES)).T
+
+
+def adjacency_kernel(n_own, starts, parts, dst_ref, col_ref, own_ref, rec_ref, acc):
+    part, tile = parts[0], pl.program_id(0)
+    lo, hi = starts[tile], starts[tile + 1]
+    own_blocks = n_own // COLS
+    n_recv = rec_ref.shape[1]
+    blocks = own_blocks + n_recv // COLS
+    dst_iota = lax.broadcasted_iota(jnp.int32, (DST_TILE, CHUNK), 0) + tile * DST_TILE
+    lane_iota = lax.broadcasted_iota(jnp.int32, (LANES, LANES), 1)
+    lanes = jnp.concatenate([lane_iota] * (CHUNK // LANES), axis=0)
+
+    def clear(b, carry):
+        acc[b] = jnp.zeros((DST_TILE, COLS), F32)
+        return carry
+
+    lax.fori_loop(0, blocks, clear, 0)
+
+    def chunk_step(c, carry):
+        to_dst = (dst_iota == dst_ref[pl.ds(c, 1), :]).astype(BF16)
+        row = col_ref[pl.ds(c, 1), :]
+        row = jnp.where(row < n_own, row, jnp.where(
+            (row >= n_own + part * n_recv) & (row < n_own + (part + 1) * n_recv), row - part * n_recv, -1))
+        columns = jnp.concatenate(
+            [as_columns(row[:, k * LANES:(k + 1) * LANES]) for k in range(CHUNK // LANES)], axis=0)
+
+        def block_step(b, carry):
+            shifted = columns - b * COLS
+            hot = jnp.concatenate([(shifted == lanes + j * LANES).astype(BF16) for j in range(COLS // LANES)], axis=1)
+            acc[b] += jnp.dot(to_dst, hot, preferred_element_type=F32)
+            return carry
+
+        return lax.fori_loop(0, blocks, block_step, carry)
+
+    lax.fori_loop(lax.div(lo, CHUNK), lax.div(hi + CHUNK - 1, CHUNK), chunk_step, 0)
+    for b in range(own_blocks):
+        own_ref[:, b * COLS:(b + 1) * COLS] = acc[b].astype(BF16)
+    for b in range(n_recv // COLS):
+        rec_ref[:, b * COLS:(b + 1) * COLS] = acc[own_blocks + b].astype(BF16)
+
+
+def adjacency(part, starts, dst_idx, columns, n_own, n_recv):
+    edges = dst_idx.shape[0]
+    grid_spec = pltpu.PrefetchScalarGridSpec(
+        num_scalar_prefetch=2, grid=(n_own // DST_TILE,),
+        in_specs=[pl.BlockSpec((edges // CHUNK, CHUNK), lambda i, *_: (0, 0))] * 2,
+        out_specs=[pl.BlockSpec((DST_TILE, n_own), lambda i, *_: (i, 0)),
+                   pl.BlockSpec((DST_TILE, n_recv), lambda i, *_: (i, 0))],
+        scratch_shapes=[pltpu.VMEM(((n_own + n_recv) // COLS, DST_TILE, COLS), F32)])
+    return pl.pallas_call(
+        functools.partial(adjacency_kernel, n_own), grid_spec=grid_spec,
+        out_shape=[jax.ShapeDtypeStruct((n_own, n_own), BF16), jax.ShapeDtypeStruct((n_own, n_recv), BF16)],
+        compiler_params=pltpu.CompilerParams(vmem_limit_bytes=VMEM_BYTES),
+        cost_estimate=pl.CostEstimate(flops=30 * 10**9, bytes_accessed=40 * 10**6, transcendentals=0),
+        name='adjacency',
+    )(starts, jnp.reshape(part, (1,)).astype(jnp.int32), dst_idx.reshape(-1, CHUNK), columns.reshape(-1, CHUNK))
+
+
+def pick_kernel(list_ref, rows_ref, out_ref):
+    n_rows = rows_ref.shape[0]
+    lane_iota = lax.broadcasted_iota(jnp.int32, (LANES, LANES), 1)
+
+    def hot(row):
+        columns = as_columns(row)
+        return jnp.concatenate(
+            [(columns == lane_iota + j * LANES).astype(BF16) for j in range(n_rows // LANES)], axis=1)
+
+    all_hot = jnp.concatenate([hot(list_ref[b:b + 1, :]) for b in range(BATCH)], axis=0)
+    picked = jnp.dot(all_hot, rows_ref[...], preferred_element_type=F32).astype(BF16)
+    for b in range(BATCH):
+        out_ref[b] = picked[b * LANES:(b + 1) * LANES]
+
+
+def pick(lists, rows):
+    group, _ = lists.shape
+    n_rows, width = rows.shape
+    return pl.pallas_call(
+        pick_kernel, grid=(group // BATCH,),
+        in_specs=[pl.BlockSpec((BATCH, LANES), lambda i: (i, 0)),
+                  pl.BlockSpec((n_rows, width), lambda i: (0, 0))],
+        out_specs=pl.BlockSpec((BATCH, LANES, width), lambda i: (i, 0, 0)),
+        out_shape=jax.ShapeDtypeStruct((group, LANES, width), BF16),
+        compiler_params=pltpu.CompilerParams(vmem_limit_bytes=VMEM_BYTES),
+        cost_estimate=pl.CostEstimate(flops=2 * group * LANES * n_rows * width, bytes_accessed=4 * 10**6,
+                                      transcendentals=0),
+        name='pick',
+    )(lists, rows)
+
+
+def put_back_kernel(list_ref, sent_ref, add_ref, out_ref):
+    n_rows = out_ref.shape[0]
+    row_iota = lax.broadcasted_iota(jnp.int32, (n_rows, LANES), 0)
+
+    @pl.when(pl.program_id(0) == 0)
+    def _():
+        out_ref[...] = add_ref[...]
+
+    hot = jnp.concatenate([(row_iota == list_ref[b:b + 1, :]).astype(BF16) for b in range(BATCH)], axis=1)
+    rows = jnp.concatenate([sent_ref[b] for b in range(BATCH)], axis=0)
+    out_ref[...] += jnp.dot(hot, rows, preferred_element_type=F32)
+
+
+def put_back(lists, sent, add):
+    group, _ = lists.shape
+    n_rows, width = add.shape
+    return pl.pallas_call(
+        put_back_kernel, grid=(group // BATCH,),
+        in_specs=[pl.BlockSpec((BATCH, LANES), lambda i: (i, 0)),
+                  pl.BlockSpec((BATCH, LANES, width), lambda i: (i, 0, 0)),
+                  pl.BlockSpec((n_rows, width), lambda i: (0, 0))],
+        out_specs=pl.BlockSpec((n_rows, width), lambda i: (0, 0)),
+        out_shape=jax.ShapeDtypeStruct((n_rows, width), F32),
+        compiler_params=pltpu.CompilerParams(vmem_limit_bytes=VMEM_BYTES),
+        cost_estimate=pl.CostEstimate(flops=2 * group * LANES * n_rows * width, bytes_accessed=8 * 10**6,
+                                      transcendentals=0),
+        name='put_back',
+    )(lists, sent, add)
+
+
+def gather_in_kernel(adj_ref, rows_ref, add_ref, out_ref):
+    out_ref[...] = add_ref[...] + jnp.dot(adj_ref[...], rows_ref[...], preferred_element_type=F32)
+
+
+def gather_in(adj_rec, rows, add):
+    n_own, n_recv = adj_rec.shape
+    width = rows.shape[1]
+    return pl.pallas_call(
+        gather_in_kernel, grid=(n_own // DST_TILE,),
+        in_specs=[pl.BlockSpec((DST_TILE, n_recv), lambda i: (i, 0)),
+                  pl.BlockSpec((n_recv, width), lambda i: (0, 0)),
+                  pl.BlockSpec((DST_TILE, width), lambda i: (i, 0))],
+        out_specs=pl.BlockSpec((DST_TILE, width), lambda i: (i, 0)),
+        out_shape=jax.ShapeDtypeStruct((n_own, width), F32),
+        compiler_params=pltpu.CompilerParams(vmem_limit_bytes=VMEM_BYTES),
+        cost_estimate=pl.CostEstimate(flops=2 * n_own * n_recv * width, bytes_accessed=20 * 10**6, transcendentals=0),
+        name='gather_in',
+    )(adj_rec, rows, add)
+
+
+def spread_out_kernel(adj_ref, rows_ref, out_ref):
+    out_ref[...] = lax.dot_general(adj_ref[...], rows_ref[...], (((0,), (0,)), ((), ())),
+                                   preferred_element_type=F32).astype(BF16)
+
+
+def spread_out(adj_rec, rows):
+    n_own, n_recv = adj_rec.shape
+    width = rows.shape[1]
+    return pl.pallas_call(
+        spread_out_kernel, grid=(n_recv // COLS,),
+        in_specs=[pl.BlockSpec((n_own, COLS), lambda i: (0, i)),
+                  pl.BlockSpec((n_own, width), lambda i: (0, 0))],
+        out_specs=pl.BlockSpec((COLS, width), lambda i: (i, 0)),
+        out_shape=jax.ShapeDtypeStruct((n_recv, width), BF16),
+        compiler_params=pltpu.CompilerParams(vmem_limit_bytes=VMEM_BYTES),
+        cost_estimate=pl.CostEstimate(flops=2 * n_own * n_recv * width, bytes_accessed=20 * 10**6, transcendentals=0),
+        name='spread_out',
+    )(adj_rec, rows)
+
+
+def before(count):
+    index = jnp.arange(count, dtype=jnp.int32)
+    return index[:, None] < index[None, :]
+
+
+def rank_in_row(flags):
+    tri = before(flags.shape[1]).astype(BF16)
+    return jnp.dot(flags.astype(BF16), tri, preferred_element_type=F32).astype(jnp.int32)
+
+
+def exchange_plan(send_idx, src_idx, n_own):
+    group, slots = send_idx.shape
+    halo = src_idx - n_own
+    peer, slot = halo // slots, halo % slots
+    from_peer = ((halo >= 0)[:, None] & (peer[:, None] == jnp.arange(group, dtype=jnp.int32)[None, :])).astype(BF16)
+    at_slot = (slot[:, None] == jnp.arange(slots, dtype=jnp.int32)[None, :]).astype(BF16)
+    needed = jnp.einsum('eg,es->gs', from_peer, at_slot, preferred_element_type=F32) > 0
+    rank = rank_in_row(needed)
+    my_rounds = (jnp.max(jnp.where(needed, rank, 0)) // LANES + 1).astype(jnp.int32)
+    upper = rank // LANES * group + jnp.arange(group, dtype=jnp.int32)[:, None]
+    split = jnp.concatenate([upper, rank % LANES], axis=1).astype(BF16)
+    found = jnp.dot(from_peer, split, preferred_element_type=F32)
+    found = jnp.sum((found[:, :slots] * LANES + found[:, slots:]) * at_slot.astype(F32), axis=1).astype(jnp.int32)
+    columns = jnp.where(halo >= 0, n_own + found, src_idx)
+    message = jnp.concatenate([jnp.where(needed, rank, -1), jnp.full((group, LANES), my_rounds)], axis=1)
+    message = lax.all_to_all(message, GROUP_AXIS, 0, 0, tiled=True)
+    asked, rounds = message[:, :slots], jnp.max(message[:, slots])
+    k = jnp.arange(slots, dtype=jnp.int32)
+    chosen = asked[:, None, :] == k[None, :, None]
+    lists = jnp.sum(jnp.where(chosen, send_idx[:, None, :] + 1, 0), axis=2) - 1
+    return columns, rounds, lists.reshape(group, slots // LANES, LANES).transpose(1, 0, 2)
 
 
 def weight_grads(h_in, neigh_mean, d_pre, d_pre_bf):
@@ -42,23 +237,45 @@
                     w_self_1, w_neigh_1, bias_1, w_self_2, w_neigh_2, bias_2,
                     w_self_3, w_neigh_3, bias_3):
         n_own = features.shape[0]
-        send_flat = send_idx.reshape(-1)
-        table_rows = n_own + send_flat.shape[0]
+        group, slots = send_idx.shape
+        columns, rounds, lists = exchange_plan(send_idx, src_idx, n_own)
+        n_recv = group * LANES
+        starts = jnp.sum(dst_idx[None, :] < (jnp.arange(n_own // DST_TILE + 1) * DST_TILE)[:, None],
+                         axis=1, dtype=jnp.int32)
+
+        def adjacency_of(part):
+            return adjacency(part, starts, dst_idx, columns, n_own, n_recv)
+
+        adj_own, adj_first = adjacency_of(0)
+
+        def swap(rows):
+            return lax.all_to_all(rows, GROUP_AXIS, 0, 0, tiled=True)
+
+        def aggregate(hidden):
+            def one_round(part, adj_rec, total):
+                received = swap(pick(lists[part], hidden))
+                return gather_in(adj_rec, received.reshape(n_recv, -1), total)
+
+            summed = one_round(0, adj_first, jnp.dot(adj_own, hidden, preferred_element_type=F32))
+            summed = lax.fori_loop(1, rounds, lambda part, total: one_round(part, adjacency_of(part)[1], total), summed)
+            return (summed * inv_deg[:, None]).astype(BF16)
 
         def layer(hidden, w_self, w_neigh, bias):
-            outgoing = jnp.take(hidden, send_flat, axis=0)
-            received = lax.all_to_all(outgoing, GROUP_AXIS, 0, 0, tiled=True)
-            table = jnp.concatenate([hidden, received], axis=0)
-            neigh_mean = aggregate(table, src_idx, dst_idx, inv_deg)
+            neigh_mean = aggregate(hidden)
             pre_act = (jnp.dot(hidden, w_self, preferred_element_type=jnp.float32)
                        + jnp.dot(neigh_mean, w_neigh, preferred_element_type=jnp.float32) + bias)
             return neigh_mean, pre_act
 
-        def back_to_owners(d_mean):
-            d_table = aggregate_grad(d_mean, src_idx, dst_idx, inv_deg, table_rows)
-            returned = lax.all_to_all(d_table[n_own:].astype(jnp.bfloat16), GROUP_AXIS, 0, 0, tiled=True)
-            owner_sum = jax.ops.segment_sum(returned.astype(jnp.float32), send_flat, num_segments=n_own)
-            return d_table[:n_own] + owner_sum
+        def back_to_owners(d_mean, d_self):
+            d_sum = (d_mean * inv_deg[:, None]).astype(BF16)
+
+            def one_round(part, adj_rec, total):
+                returned = swap(spread_out(adj_rec, d_sum).reshape(group, LANES, -1))
+                return put_back(lists[part], returned, total)
+
+            d_own = d_self + jnp.einsum('nt,nd->td', adj_own, d_sum, preferred_element_type=F32)
+            return lax.fori_loop(1, rounds, lambda part, total: one_round(part, adjacency_of(part)[1], total),
+                                 one_round(0, adj_first, d_own))
 
         mean_1, pre_1 = layer(features, w_self_1, w_neigh_1, bias_1)
         hidden_1 = jax.nn.relu(pre_1).astype(jnp.bfloat16)
@@ -72,11 +289,11 @@
         d_bf_3 = d_pre_3.astype(jnp.bfloat16)
         g_self_3, g_neigh_3, g_bias_3 = weight_grads(hidden_2, mean_3, d_pre_3, d_bf_3)
         d_self_3, d_mean_3 = input_grads(d_bf_3, w_self_3, w_neigh_3)
-        d_pre_2 = jnp.where(pre_2 > 0, d_self_3 + back_to_owners(d_mean_3), 0.0)
+        d_pre_2 = jnp.where(pre_2 > 0, back_to_owners(d_mean_3, d_self_3), 0.0)
         d_bf_2 = d_pre_2.astype(jnp.bfloat16)
         g_self_2, g_neigh_2, g_bias_2 = weight_grads(hidden_1, mean_2, d_pre_2, d_bf_2)
         d_self_2, d_mean_2 = input_grads(d_bf_2, w_self_2, w_neigh_2)
-        d_pre_1 = jnp.where(pre_1 > 0, d_self_2 + back_to_owners(d_mean_2), 0.0)
+        d_pre_1 = jnp.where(pre_1 > 0, back_to_owners(d_mean_2, d_self_2), 0.0)
         d_bf_1 = d_pre_1.astype(jnp.bfloat16)
         g_self_1, g_neigh_1, g_bias_1 = weight_grads(features, mean_1, d_pre_1, d_bf_1)
 

time: 2050 us -> 826 us (0.40)
  waiting for transfers between devices: 1050 us -> 421 us
  other arithmetic: 637 us -> 21.6 us
  local copies, waits for them, and re-layouts: 220 us -> 22 us
  Pallas kernels: 0 us -> 193 us
  matrix products: 33.8 us -> 67.8 us
    all_to_all x5 -> x6, waiting for transfers between devices: 778 us -> 161 us  [the longest x5 155 us: swap(): return lax.all_to_all(rows, GROUP_AXIS, 0, 0, tiled=True)]
    scatter-add x7 -> x0, other arithmetic: 567 us -> none  [the longest x3 229 us: aggregate(): jax.ops.segment_sum(gathered, dst_idx, num_segments=inv_deg.shape[0], ind...]
    pallas_call x0 -> x11, Pallas kernels: none -> 193 us  [the longest x1 100 us: adjacency(): pl.pallas_call(functools.partial(adjacency_kernel, n_own), grid_spec=grid...]
    gather x3 -> x0, local copies, waits for them, and re-layouts: 186 us -> none  [layer(): outgoing = jnp.take(hidden, send_flat, axis=0)]
    dot_general x0 -> x8, matrix products: none -> 39.5 us  [the longest x3 20.8 us: aggregate(): jnp.dot(adj_own, hidden, preferred_element_type=F32)]
    concatenate x3 -> x0, other arithmetic: 32.7 us -> none  [layer(): table = jnp.concatenate([hidden, received], axis=0)]
    select_n x4 -> x2, other arithmetic: 23.7 us -> 0.81 us  [the longest x1 0.8 us: exchange_plan(): peer, slot = (halo // slots, halo % slots)]
    all_to_all x5 -> x6, starting transfers between devices: 43.8 us -> 29.7 us  [the longest x5 22.1 us: swap(): return lax.all_to_all(rows, GROUP_AXIS, 0, 0, tiled=True)]
  transfers between devices with their start and end apart: 7 -> 8, of which waited for: 7 -> 7; matrix products, arithmetic and copies ran while one was open for 1% -> 7% of each run, Pallas kernels for 0% -> 12%
where the time goes in v1:
time: 826 us; the launch traced here: 818 us
  waiting for transfers between devices  421 us (51%)
  Pallas kernels  193 us (23%)
  matrix products  67.8 us (8%)
  blocking collectives  38.2 us (5%)
  starting transfers between devices  30 us (4%)
  local copies, waits for them, and re-layouts  22 us (3%)
  other arithmetic  21.6 us (3%)
  between operations  20.4 us (2%)
    psum x2, waiting for transfers between devices, device_step(): lax.psum((g_self_1, g_neigh_1, g_bias_1, g_self_2, g_neigh_2, g_bias_2, g...  260 us
    all_to_all x5, waiting for transfers between devices, swap(): return lax.all_to_all(rows, GROUP_AXIS, 0, 0, tiled=True)  155 us
    pallas_call x1, Pallas kernels, adjacency(): pl.pallas_call(functools.partial(adjacency_kernel, n_own), grid_spec=grid...  100 us
    psum x1, blocking collectives, device_step(): totals = lax.psum(jnp.stack([loss_sum, jnp.sum(train_mask)]), GROUP_AXIS)  38.2 us
    pallas_call x3, Pallas kernels, gather_in(): pl.pallas_call(gather_in_kernel, grid=(n_own // DST_TILE,), in_specs=[pl....  35.2 us
    pallas_call x2, Pallas kernels, spread_out(): pl.pallas_call(spread_out_kernel, grid=(n_recv // COLS,), in_specs=[pl.Bl...  23.7 us
    all_to_all x5, starting transfers between devices, swap(): return lax.all_to_all(rows, GROUP_AXIS, 0, 0, tiled=True)  22.1 us
    dot_general x3, matrix products, aggregate(): jnp.dot(adj_own, hidden, preferred_element_type=F32)  20.8 us
  transfers between devices with their start and end apart: 8, of which 7 were waited for; matrix products, arithmetic and copies ran while one was open for 7% of the time, Pallas kernels for 12%

profile of v1, /device:TPU:0, one launch (start us, length us, event | category | flops | bytes accessed | tf_op | source)
XLA Modules:
  0.0 817.9 jit_solution(16432470301078635322)
XLA Ops:
  8.7 2.3 fusion.10
  15.3 3.5 fusion.16
  18.8 2.9 fusion.1
  21.7 7.6 all-to-all-start.5
  30.8 5.9 all-to-all-done.5
  36.7 4.2 select_reduce_fusion
  41.5 6.6 pick.6
  48.1 2.6 all-to-all-start.6
  50.7 100.1 %adjacency.6 = (bf16[2048,2048]{1,0:T(8,128)(2,1)}, bf16[2048,4096]{1,0:T(8,128)(2,1)}) custom-call(s32[9]{0:T(128)S(1)} %convert_reduce_fusion.starts, s32[1]{0:T(128)} %constant.112.clone.1.parts, s32[24,256]{1,0:T(8,128)} %reshape.129.dst_ref, s32[24,256]{1,0:T(8,128)} %reshape.130.col_ref), custom_call_target="tpu_custom_call" | custom-call | flops 30000001024 | bytes 40000000 | tf_op jit(solution)/shard_map/adjacency/pallas_call | solution.py:72
  150.9 1.8 fusion.42
  152.7 6.7 fusion.43.add_ref
  161.0 10.7 %gather_in.6 = f32[2048,128]{1,0:T(8,128)S(1)} custom-call(bf16[2048,4096]{1,0:T(8,128)(2,1)} %get-tuple-element.232.adj_ref, bf16[4096,128]{1,0:T(8,128)(2,1)} %bitcast.136, f32[2048,128]{1,0:T(8,128)} %fusion.43.add_ref), custom_call_target="tpu_custom_call" | custom-call | flops 2147483648 | bytes 20000000 | tf_op jit(solution)/shard_map/gather_in/pallas_call | solution.py:149
  171.8 1.1 while.55
  172.9 3.8 maximum_convert_fusion.1
  176.7 6.7 pick.7
  183.4 5.8 all-to-all-start.7
  189.3 1.8 fusion.44
  191.1 7.0 fusion.45.add_ref
  198.2 39.8 %all-to-all-done.7 = bf16[32,128,256]{2,1,0:T(8,128)(2,1)S(1)} async-done(((bf16[32,128,256]{2,1,0:T(8,128)(2,1)}), bf16[32,128,256]{2,1,0:T(8,128)(2,1)S(1)}, u32[]{:S(2)}, u32[]{:S(2)}) %all-to-all-start.7) | async-done | bytes 2097184 | tf_op jit(solution)/shard_map/all_to_all | solution.py:252
  237.9 1.4 copy-done.16
  239.3 12.3 %gather_in.7 = f32[2048,256]{1,0:T(8,128)} custom-call(bf16[2048,4096]{1,0:T(8,128)(2,1)} %get-tuple-element.232.adj_ref, bf16[4096,256]{1,0:T(8,128)(2,1)} %bitcast.134, f32[2048,256]{1,0:T(8,128)} %fusion.45.add_ref), custom_call_target="tpu_custom_call" | custom-call | flops 4294967296 | bytes 20000000 | tf_op jit(solution)/shard_map/gather_in/pallas_call | solution.py:149
  253.2 4.1 maximum_convert_fusion
  257.4 6.7 pick.8
  264.1 4.2 all-to-all-start.8
  268.3 1.1 fusion.46
  269.5 7.1 fusion.47.add_ref
  276.5 40.4 %all-to-all-done.8 = bf16[32,128,256]{2,1,0:T(8,128)(2,1)S(1)} async-done(((bf16[32,128,256]{2,1,0:T(8,128)(2,1)}), bf16[32,128,256]{2,1,0:T(8,128)(2,1)S(1)}, u32[]{:S(2)}, u32[]{:S(2)}) %all-to-all-start.8) | async-done | bytes 2097184 | tf_op jit(solution)/shard_map/all_to_all | solution.py:252
  316.9 1.3 copy-done.17
  318.2 12.3 %gather_in.8 = f32[2048,256]{1,0:T(8,128)} custom-call(bf16[2048,4096]{1,0:T(8,128)(2,1)} %get-tuple-element.232.adj_ref, bf16[4096,256]{1,0:T(8,128)(2,1)} %bitcast.135, f32[2048,256]{1,0:T(8,128)} %fusion.47.add_ref), custom_call_target="tpu_custom_call" | custom-call | flops 4294967296 | bytes 20000000 | tf_op jit(solution)/shard_map/gather_in/pallas_call | solution.py:149
  331.3 2.5 fusion.41
  334.5 1.4 pad_maximum_fusion
  335.9 38.2 %psum.70 = f32[2]{0:T(128)S(1)} all-reduce(f32[2]{0:T(128)S(1)} %pad_maximum_fusion), channel_id=1, replica_groups=mesh['gp'=32] {'gp'}, use_global_device_ids=true, to_apply=%region_16.17 | all-reduce | flops 2 | bytes 16 | tf_op jit(solution)/shard_map/psum | solution.py:286
  374.7 1.5 fusion.34
  376.6 12.0 %spread_out.4 = bf16[4096,256]{1,0:T(8,128)(2,1)} custom-call(bf16[2048,4096]{1,0:T(8,128)(2,1)} %get-tuple-element.232.adj_ref, bf16[2048,256]{1,0:T(8,128)(2,1)S(1)} %fusion.8.rows_ref), custom_call_target="tpu_custom_call" | custom-call | flops 4294967296 | bytes 20000000 | tf_op jit(solution)/shard_map/spread_out/pallas_call | solution.py:170
  388.7 5.4 all-to-all-start.9
  394.2 6.0 fusion.48
  400.2 1.8 convolution_add_fusion.add_ref
  402.0 40.8 %all-to-all-done.9.sent_ref = bf16[32,128,256]{2,1,0:T(8,128)(2,1)} async-done(((bf16[32,128,256]{2,1,0:T(8,128)(2,1)}), bf16[32,128,256]{2,1,0:T(8,128)(2,1)}, u32[]{:S(2)}, u32[]{:S(2)}) %all-to-all-start.9) | async-done | bytes 2097184 | tf_op jit(solution)/shard_map/all_to_all | solution.py:252
  442.8 7.0 put_back.4
  450.5 2.7 fusion.14
  454.7 11.7 %spread_out.5 = bf16[4096,256]{1,0:T(8,128)(2,1)} custom-call(bf16[2048,4096]{1,0:T(8,128)(2,1)} %get-tuple-element.232.adj_ref, bf16[2048,256]{1,0:T(8,128)(2,1)S(1)} %fusion.7.rows_ref), custom_call_target="tpu_custom_call" | custom-call | flops 4294967296 | bytes 20000000 | tf_op jit(solution)/shard_map/spread_out/pallas_call | solution.py:170
  466.4 4.1 all-to-all-start.10
  470.9 2.3 fusion.51
  474.2 1.2 fusion.50
  475.4 1.6 fusion.38
  477.0 6.0 fusion.49
  483.0 1.8 convolution_add_fusion.1.add_ref
  484.8 34.2 %all-to-all-done.10.sent_ref = bf16[32,128,256]{2,1,0:T(8,128)(2,1)} async-done(((bf16[32,128,256]{2,1,0:T(8,128)(2,1)}), bf16[32,128,256]{2,1,0:T(8,128)(2,1)}, u32[]{:S(2)}, u32[]{:S(2)}) %all-to-all-start.10) | async-done | bytes 2097184 | tf_op jit(solution)/shard_map/all_to_all | solution.py:252
  519.0 7.0 put_back.5
  526.7 2.0 fusion.12
  528.8 1.4 fusion.37
  530.1 1.1 convolution_bitcast_fusion
  531.3 3.9 fusion.11
  536.6 125.1 %all-reduce.8.cloned.1.call-done = (f32[128,256]{0,1:T(8,128)}, f32[128,256]{1,0:T(8,128)}, f32[256,256]{1,0:T(8,128)}, f32[256,256]{1,0:T(8,128)}) async-done(((f32[128,256]{0,1:T(8,128)}, f32[128,256]{1,0:T(8,128)}, f32[256,256]{1,0:T(8,128)}, f32[256,256]{1,0:T(8,128)}), (f32[128,256]{0,1:T(8,128)}, f32[128,256]{1,0:T(8,128)}, f32[256,256]{1,0:T(8,128)}, ...) | async-done | bytes 786448 | tf_op jit(solution)/shard_map/psum | solution.py:300
  661.8 1.7 copy.34
  663.4 134.8 %all-reduce.6.cloned.1.call-done = (f32[256]{0:T(256)}, f32[256]{0:T(256)}, f32[256,40]{0,1:T(8,128)}, f32[256,40]{0,1:T(8,128)}, f32[40]{0:T(128)}) async-done(((f32[256]{0:T(256)}, f32[256]{0:T(256)}, f32[256,40]{0,1:T(8,128)}, f32[256,40]{0,1:T(8,128)}, f32[40]{0:T(128)}), (f32[256]{0:T(256)}, f32[256]{0:T(256)}, f32[256,40]{0,1:T(8,128)}, f32[256,40]{0,1:T(8,128)}, ...) | async-done | bytes 84144 | tf_op jit(solution)/shard_map/psum | solution.py:300
  798.2 1.6 copy.92
  799.8 1.2 copy.93
  801.0 1.7 copy.94
  802.7 1.7 copy.95
  804.3 1.2 copy.96
  805.6 1.4 copy.97
  807.0 1.4 copy.98
  808.4 1.1 copy.99
  (141 shorter events, 15.6 us)
Async XLA Ops:
  7.2 246.1 %copy-start = (bf16[256,256]{1,0:T(8,128)(2,1)S(1)}, bf16[256,256]{1,0:T(8,128)(2,1)}, u32[]{:S(2)}) copy-start(bf16[256,256]{1,0:T(8,128)(2,1)} %param.37) | copy-start | bytes 393220
  8.7 6.6 copy-start.46
  18.8 2.9 copy-start.41
  18.8 11.1 %copy-start.24 = (s32[6144]{0:T(1024)S(1)}, s32[6144]{0:T(1024)}, u32[]{:S(2)}) copy-start(s32[6144]{0:T(1024)} %param.31) | copy-start | bytes 73732
  18.8 22.7 %copy-start.22 = (bf16[2048,128]{1,0:T(8,128)(2,1)S(1)}, bf16[2048,128]{1,0:T(8,128)(2,1)}, u32[]{:S(2)}) copy-start(bf16[2048,128]{1,0:T(8,128)(2,1)} %rows_ref.1) | copy-start | bytes 1572868
  21.7 129.1 %copy-start.29 = (s32[6144]{0:T(1024)}, s32[6144]{0:T(1024)S(1)}, u32[]{:S(2)}) copy-start(s32[6144]{0:T(1024)S(1)} %add_select_fusion.4) | copy-start | bytes 73732
  21.7 15.0 %all-to-all-start.5 = ((s32[32,1,640]{2,1,0:T(1,128)}), s32[32,1,640]{2,1,0:T(1,128)S(1)}, u32[]{:S(2)}, u32[]{:S(2)}) async-start(s32[32,1,640]{2,1,0:T(1,128)} %copy.32), calls=%async_computation.5 | async-start | bytes 163840 | tf_op jit(solution)/shard_map/all_to_all | solution.py:207
  48.1 111.9 %all-to-all-start.6 = ((bf16[32,128,128]{2,1,0:T(8,128)(2,1)}), bf16[32,128,128]{2,1,0:T(8,128)(2,1)S(1)}, u32[]{:S(2)}, u32[]{:S(2)}) async-start(bf16[32,128,128]{2,1,0:T(8,128)(2,1)} %pick.6), calls=%async_computation.6 | async-start | bytes 2097152 | tf_op jit(solution)/shard_map/all_to_all | solution.py:252
  50.7 100.2 %copy-start.47 = (bf16[128,256]{1,0:T(8,128)(2,1)S(1)}, bf16[128,256]{1,0:T(8,128)(2,1)}, u32[]{:S(2)}) copy-start(bf16[128,256]{1,0:T(8,128)(2,1)} %param.33) | copy-start | bytes 196612
  160.0 1.0 copy-start.18
  171.7 1.1 copy-start.34
  171.7 1.1 copy-start.45
  171.7 1.1 copy-start.51
  172.9 3.8 copy-start.7
  183.4 5.8 copy-start.30
  183.4 5.9 copy-start.25
  183.4 5.9 copy-start.39
  183.4 54.5 %all-to-all-start.7 = ((bf16[32,128,256]{2,1,0:T(8,128)(2,1)}), bf16[32,128,256]{2,1,0:T(8,128)(2,1)S(1)}, u32[]{:S(2)}, u32[]{:S(2)}) async-start(bf16[32,128,256]{2,1,0:T(8,128)(2,1)} %pick.7), calls=%async_computation.7 | async-start | bytes 4194304 | tf_op jit(solution)/shard_map/all_to_all | solution.py:252
  237.9 1.4 copy-start.16
  251.6 1.7 copy-start.35
  251.6 1.7 copy-start.50
  252.3 1.0 copy-start.14
  264.1 4.2 copy-start.31
  264.1 4.2 copy-start.26
  264.1 4.2 copy-start.43
  264.1 52.8 %all-to-all-start.8 = ((bf16[32,128,256]{2,1,0:T(8,128)(2,1)}), bf16[32,128,256]{2,1,0:T(8,128)(2,1)S(1)}, u32[]{:S(2)}, u32[]{:S(2)}) async-start(bf16[32,128,256]{2,1,0:T(8,128)(2,1)} %pick.8), calls=%async_computation.8 | async-start | bytes 4194304 | tf_op jit(solution)/shard_map/all_to_all | solution.py:252
  316.9 1.3 copy-start.17
  330.5 0.7 copy-start.36
  330.5 0.8 copy-start.42
  330.5 0.8 copy-start.52
  331.2 45.4 %copy-start.13 = (bf16[2048,256]{1,0:T(8,128)(2,1)}, bf16[2048,256]{1,0:T(8,128)(2,1)S(1)}, u32[]{:S(2)}) copy-start(bf16[2048,256]{1,0:T(8,128)(2,1)S(1)} %get-tuple-element.1109) | copy-start | bytes 3145732
  331.2 2.6 copy-start.48
  331.2 2.7 copy-start.49
  376.1 24.0 %copy-start.19 = (bf16[2048,40]{0,1:T(8,128)(2,1)}, bf16[2048,40]{0,1:T(8,128)(2,1)S(1)}, u32[]{:S(2)}) copy-start(bf16[2048,40]{0,1:T(8,128)(2,1)S(1)} %get-tuple-element.371) | copy-start | bytes 491524
  376.6 17.5 %copy-start.9 = (bf16[2048,256]{1,0:T(8,128)(2,1)}, bf16[2048,256]{1,0:T(8,128)(2,1)S(1)}, u32[]{:S(2)}) copy-start(bf16[2048,256]{1,0:T(8,128)(2,1)S(1)} %fusion.8.rows_ref) | copy-start | bytes 3145732
  388.7 5.4 copy-start.32
  388.7 5.4 copy-start.27
  388.7 54.1 %all-to-all-start.9 = ((bf16[32,128,256]{2,1,0:T(8,128)(2,1)}), bf16[32,128,256]{2,1,0:T(8,128)(2,1)}, u32[]{:S(2)}, u32[]{:S(2)}) async-start(bf16[32,128,256]{2,1,0:T(8,128)(2,1)} %bitcast.133), calls=%async_computation.9 | async-start | bytes 4194304 | tf_op jit(solution)/shard_map/all_to_all | solution.py:252
  394.1 6.0 copy-start.44
  402.0 47.9 %copy-start.10 = (bf16[2048,256]{1,0:T(8,128)(2,1)S(1)}, bf16[2048,256]{1,0:T(8,128)(2,1)}, u32[]{:S(2)}) copy-start(bf16[2048,256]{1,0:T(8,128)(2,1)} %copy-done.9) | copy-start | bytes 3145732
  450.5 2.7 copy-start.6
  450.5 2.7 copy-start.21
  450.5 3.7 copy-start.37
  453.2 1.0 copy-start.11
  466.4 4.4 copy-start.33
  466.4 4.4 copy-start.28
  466.4 4.5 copy-start.20
  466.4 6.8 copy-start.4
  466.4 52.6 %all-to-all-start.10 = ((bf16[32,128,256]{2,1,0:T(8,128)(2,1)}), bf16[32,128,256]{2,1,0:T(8,128)(2,1)}, u32[]{:S(2)}, u32[]{:S(2)}) async-start(bf16[32,128,256]{2,1,0:T(8,128)(2,1)} %bitcast.132), calls=%async_computation.10 | async-start | bytes 4194304 | tf_op jit(solution)/shard_map/all_to_all | solution.py:252
  470.5 191.3 %all-reduce.8.cloned.1.call-start = ((), (), s32[]{:S(2)}) async-start(), calls=%async_computation.12 | async-start | bytes 1572864 | tf_op jit(solution)/shard_map/psum | solution.py:300
  470.9 3.4 copy-start.12
  470.9 3.4 copy-start.15
  473.2 2.3 copy-start.3
  477.0 6.0 copy-start.40
  526.7 2.0 copy-start.8
  526.7 2.0 copy-start.38
  528.7 1.4 copy-start.23
  531.3 267.0 %all-reduce.6.cloned.1.call-start = ((), (), s32[]{:S(2)}) async-start(), calls=%async_computation.11 | async-start | bytes 168960 | tf_op jit(solution)/shard_map/psum | solution.py:300
Sparse Core Ops, SparseCore 0:
  531.4 130.3 all-reduce.7
  669.3 128.8 all-reduce.5

commit v2 on v1

--- a/solution.py
+++ b/solution.py
@@ -10,11 +10,13 @@
 GROUP_AXIS = 'gp'
 LANES = 128
 DST_TILE = 256
-CHUNK = 256
+WINDOW = 8
 COLS = 512
 BATCH = 8
 VMEM_BYTES = 60 * 1024 * 1024
+MESH = pl.DeviceIdType.MESH
 F32 = jnp.float32
+IDX = jnp.int16
 BF16 = jnp.bfloat16
 
 
@@ -22,60 +24,70 @@
     return jnp.broadcast_to(row, (LANES, LANES)).T
 
 
-def adjacency_kernel(n_own, starts, parts, dst_ref, col_ref, own_ref, rec_ref, acc):
+def adjacency_kernel(n_own, starts, parts, dst_ref, col_ref, own_ref, rec_ref):
     part, tile = parts[0], pl.program_id(0)
-    lo, hi = starts[tile], starts[tile + 1]
-    own_blocks = n_own // COLS
+    first = lax.div(starts[tile], LANES)
+    last = lax.div(starts[tile + 1] + LANES - 1, LANES)
     n_recv = rec_ref.shape[1]
-    blocks = own_blocks + n_recv // COLS
-    dst_iota = lax.broadcasted_iota(jnp.int32, (DST_TILE, CHUNK), 0) + tile * DST_TILE
-    lane_iota = lax.broadcasted_iota(jnp.int32, (LANES, LANES), 1)
-    lanes = jnp.concatenate([lane_iota] * (CHUNK // LANES), axis=0)
-
-    def clear(b, carry):
-        acc[b] = jnp.zeros((DST_TILE, COLS), F32)
+    dst_iota = lax.broadcasted_iota(jnp.int32, (DST_TILE, LANES), 0) + tile * DST_TILE
+    lanes = lax.broadcasted_iota(jnp.int32, (WINDOW * LANES, LANES), 1).astype(IDX)
+
+    def window_step(w, carry):
+        rows = first + w * WINDOW
+        dst = dst_ref[pl.ds(rows, WINDOW), :]
+        col = col_ref[pl.ds(rows, WINDOW), :]
+        mine = (col >= n_own + part * n_recv) & (col < n_own + (part + 1) * n_recv)
+        col = jnp.where(col < n_own, col, jnp.where(mine, col - part * n_recv, -1))
+        to_dst = jnp.concatenate([(dst_iota == dst[k:k + 1, :]).astype(BF16) for k in range(WINDOW)], axis=1)
+        columns = jnp.concatenate([as_columns(col[k:k + 1, :]) for k in range(WINDOW)], axis=0).astype(IDX)
+
+        def fill(out_ref, base):
+            def block_step(b, carry):
+                offset = pl.multiple_of(b * COLS, COLS)
+                shifted = columns - (base + offset).astype(IDX)
+                hot = jnp.concatenate([jnp.where(shifted == lanes + IDX(j * LANES), BF16(1), BF16(0))
+                                       for j in range(COLS // LANES)], axis=1)
+                counts = jnp.dot(to_dst, hot, preferred_element_type=F32)
+                at = (slice(None), pl.ds(offset, COLS))
+
+                @pl.when(w == 0)
+                def _():
+                    out_ref[at] = counts.astype(BF16)
+
+                @pl.when(w > 0)
+                def _():
+                    out_ref[at] = (out_ref[at].astype(F32) + counts).astype(BF16)
+
+                return carry
+
+            lax.fori_loop(0, out_ref.shape[1] // COLS, block_step, 0)
+
+        fill(own_ref, 0)
+        fill(rec_ref, n_own)
         return carry
 
-    lax.fori_loop(0, blocks, clear, 0)
-
-    def chunk_step(c, carry):
-        to_dst = (dst_iota == dst_ref[pl.ds(c, 1), :]).astype(BF16)
-        row = col_ref[pl.ds(c, 1), :]
-        row = jnp.where(row < n_own, row, jnp.where(
-            (row >= n_own + part * n_recv) & (row < n_own + (part + 1) * n_recv), row - part * n_recv, -1))
-        columns = jnp.concatenate(
-            [as_columns(row[:, k * LANES:(k + 1) * LANES]) for k in range(CHUNK // LANES)], axis=0)
-
-        def block_step(b, carry):
-            shifted = columns - b * COLS
-            hot = jnp.concatenate([(shifted == lanes + j * LANES).astype(BF16) for j in range(COLS // LANES)], axis=1)
-            acc[b] += jnp.dot(to_dst, hot, preferred_element_type=F32)
-            return carry
-
-        return lax.fori_loop(0, blocks, block_step, carry)
-
-    lax.fori_loop(lax.div(lo, CHUNK), lax.div(hi + CHUNK - 1, CHUNK), chunk_step, 0)
-    for b in range(own_blocks):
-        own_ref[:, b * COLS:(b + 1) * COLS] = acc[b].astype(BF16)
-    for b in range(n_recv // COLS):
-        rec_ref[:, b * COLS:(b + 1) * COLS] = acc[own_blocks + b].astype(BF16)
+    windows = jnp.maximum(lax.div(last - first + WINDOW - 1, WINDOW), 1)
+    lax.fori_loop(0, windows, window_step, 0)
 
 
 def adjacency(part, starts, dst_idx, columns, n_own, n_recv):
-    edges = dst_idx.shape[0]
+    def rows_of(index):
+        padding = jnp.full((WINDOW * LANES,), -1, jnp.int32)
+        return jnp.concatenate([index, padding]).reshape(-1, LANES)
+
+    rows = dst_idx.shape[0] // LANES + WINDOW
     grid_spec = pltpu.PrefetchScalarGridSpec(
         num_scalar_prefetch=2, grid=(n_own // DST_TILE,),
-        in_specs=[pl.BlockSpec((edges // CHUNK, CHUNK), lambda i, *_: (0, 0))] * 2,
+        in_specs=[pl.BlockSpec((rows, LANES), lambda i, *_: (0, 0))] * 2,
         out_specs=[pl.BlockSpec((DST_TILE, n_own), lambda i, *_: (i, 0)),
-                   pl.BlockSpec((DST_TILE, n_recv), lambda i, *_: (i, 0))],
-        scratch_shapes=[pltpu.VMEM(((n_own + n_recv) // COLS, DST_TILE, COLS), F32)])
+                   pl.BlockSpec((DST_TILE, n_recv), lambda i, *_: (i, 0))])
     return pl.pallas_call(
         functools.partial(adjacency_kernel, n_own), grid_spec=grid_spec,
         out_shape=[jax.ShapeDtypeStruct((n_own, n_own), BF16), jax.ShapeDtypeStruct((n_own, n_recv), BF16)],
         compiler_params=pltpu.CompilerParams(vmem_limit_bytes=VMEM_BYTES),
         cost_estimate=pl.CostEstimate(flops=30 * 10**9, bytes_accessed=40 * 10**6, transcendentals=0),
         name='adjacency',
-    )(starts, jnp.reshape(part, (1,)).astype(jnp.int32), dst_idx.reshape(-1, CHUNK), columns.reshape(-1, CHUNK))
+    )(starts, jnp.reshape(part, (1,)).astype(jnp.int32), rows_of(dst_idx), rows_of(columns))
 
 
 def pick_kernel(list_ref, rows_ref, out_ref):
@@ -179,6 +191,113 @@
     )(adj_rec, rows)
 
 
+def add_up_kernel(n_chips, rows, *refs):
+    parts, (out_ref, packed, partner_half, mine, inbox, total, gathered, send, recv) = refs[:-9], refs[-9:]
+    me = lax.axis_index(GROUP_AXIS)
+    core, chip = lax.rem(me, 2), lax.div(me, 2)
+    partner = me + 1 - 2 * core
+
+    def twin(step):
+        return 2 * lax.rem(chip + step, n_chips) + core
+
+    barrier = pltpu.get_barrier_semaphore()
+    pl.semaphore_signal(barrier, inc=1, device_id=(partner,), device_id_type=MESH)
+    for step in range(1, n_chips):
+        pl.semaphore_signal(barrier, inc=1, device_id=(twin(step),), device_id_type=MESH)
+
+    at = 0
+    for ref in parts:
+        count, width = ref.shape
+        for j in range(width // LANES):
+            packed[at:at + count, :] = ref[:, j * LANES:(j + 1) * LANES]
+            at += count
+    packed[at:, :] = jnp.zeros((packed.shape[0] - at, LANES), F32)
+    half = n_chips * rows
+
+    def half_of(which):
+        return pl.ds(pl.multiple_of(which * half, 8), half)
+
+    def copy(src, dst, slot, device):
+        return pltpu.make_async_remote_copy(
+            src_ref=src, dst_ref=dst, send_sem=send.at[slot], recv_sem=recv.at[slot],
+            device_id=(device,), device_id_type=MESH)
+
+    pl.semaphore_wait(barrier, n_chips)
+    first = copy(packed.at[half_of(1 - core)], partner_half, 0, partner)
+    first.start()
+    first.wait()
+    mine[...] = (packed[half_of(core), :] + partner_half[...]).reshape(n_chips, rows, LANES)
+    sends = []
+    for step in range(1, n_chips):
+        sends.append(copy(mine.at[lax.rem(chip + step, n_chips)], inbox.at[step], step, twin(step)))
+        sends[-1].start()
+    value = mine[chip]
+    for step in range(1, n_chips):
+        sends[step - 1].wait_recv()
+        value = value + inbox[step]
+    total[...] = value
+    for item in sends:
+        item.wait_send()
+    spread = []
+    for step in range(1, n_chips):
+        spread.append(copy(total, gathered.at[core, chip], n_chips + step, twin(step)))
+        spread[-1].start()
+    gathered[core, chip] = value
+    for item in spread:
+        item.wait()
+    last = copy(gathered.at[core], gathered.at[core], 2 * n_chips, partner)
+    last.start()
+    last.wait()
+    out_ref[...] = gathered[...].reshape(2 * half, LANES)
+
+
+def add_up(parts, group):
+    n_chips = group // 2
+    used = sum(p.size for p in parts) // LANES
+    rows = -(-used // (group * 8)) * 8
+    total = group * rows
+    chunk = (rows, LANES)
+    return pl.pallas_call(
+        functools.partial(add_up_kernel, n_chips, rows),
+        in_specs=[pl.BlockSpec(memory_space=pltpu.VMEM)] * len(parts),
+        out_specs=pl.BlockSpec(memory_space=pltpu.VMEM),
+        out_shape=jax.ShapeDtypeStruct((total, LANES), F32),
+        scratch_shapes=[pltpu.VMEM((total, LANES), F32), pltpu.VMEM((total // 2, LANES), F32),
+                        pltpu.VMEM((n_chips,) + chunk, F32), pltpu.VMEM((n_chips,) + chunk, F32),
+                        pltpu.VMEM(chunk, F32), pltpu.VMEM((2, n_chips) + chunk, F32),
+                        pltpu.SemaphoreType.DMA((2 * n_chips + 1,)), pltpu.SemaphoreType.DMA((2 * n_chips + 1,))],
+        compiler_params=pltpu.CompilerParams(collective_id=0, has_side_effects=True),
+        name='add_up',
+    )(*parts)
+
+
+def unpack_kernel(flipped, packed_ref, *out_refs):
+    at = 0
+    for ref, flip in zip(out_refs[:-1], flipped):
+        count, width = ref.shape[::-1] if flip else ref.shape
+        pieces = []
+        for j in range(width // LANES):
+            pieces.append(packed_ref[at:at + count, :])
+            at += count
+        if flip:
+            short = jnp.zeros((LANES - count, LANES), F32)
+            for j, piece in enumerate(pieces):
+                ref[j * LANES:(j + 1) * LANES, :] = jnp.concatenate([piece, short], axis=0).T[:, :count]
+        else:
+            ref[...] = jnp.concatenate(pieces, axis=1)
+    out_refs[-1][...] = packed_ref[at:at + out_refs[-1].shape[0], :]
+
+
+def unpack(packed, shapes, flipped):
+    return pl.pallas_call(
+        functools.partial(unpack_kernel, flipped),
+        in_specs=[pl.BlockSpec(memory_space=pltpu.VMEM)],
+        out_specs=[pl.BlockSpec(memory_space=pltpu.VMEM)] * (len(shapes) + 1),
+        out_shape=[jax.ShapeDtypeStruct(shape, F32) for shape in shapes + ((8, LANES),)],
+        name='unpack',
+    )(packed)
+
+
 def before(count):
     index = jnp.arange(count, dtype=jnp.int32)
     return index[:, None] < index[None, :]
@@ -189,7 +308,7 @@
     return jnp.dot(flags.astype(BF16), tri, preferred_element_type=F32).astype(jnp.int32)
 
 
-def exchange_plan(send_idx, src_idx, n_own):
+def exchange_plan(send_idx, src_idx, train_mask, n_own):
     group, slots = send_idx.shape
     halo = src_idx - n_own
     peer, slot = halo // slots, halo % slots
@@ -203,13 +322,16 @@
     found = jnp.dot(from_peer, split, preferred_element_type=F32)
     found = jnp.sum((found[:, :slots] * LANES + found[:, slots:]) * at_slot.astype(F32), axis=1).astype(jnp.int32)
     columns = jnp.where(halo >= 0, n_own + found, src_idx)
-    message = jnp.concatenate([jnp.where(needed, rank, -1), jnp.full((group, LANES), my_rounds)], axis=1)
+    my_count = jnp.sum(train_mask).astype(jnp.int32)
+    extras = jnp.where(jnp.arange(LANES) == 0, my_rounds, my_count)
+    message = jnp.concatenate([jnp.where(needed, rank, -1), jnp.broadcast_to(extras, (group, LANES))], axis=1)
     message = lax.all_to_all(message, GROUP_AXIS, 0, 0, tiled=True)
     asked, rounds = message[:, :slots], jnp.max(message[:, slots])
+    count = jnp.sum(message[:, slots + 1]).astype(F32)
     k = jnp.arange(slots, dtype=jnp.int32)
     chosen = asked[:, None, :] == k[None, :, None]
     lists = jnp.sum(jnp.where(chosen, send_idx[:, None, :] + 1, 0), axis=2) - 1
-    return columns, rounds, lists.reshape(group, slots // LANES, LANES).transpose(1, 0, 2)
+    return columns, rounds, count, lists.reshape(group, slots // LANES, LANES).transpose(1, 0, 2)
 
 
 def weight_grads(h_in, neigh_mean, d_pre, d_pre_bf):
@@ -238,7 +360,7 @@
                     w_self_3, w_neigh_3, bias_3):
         n_own = features.shape[0]
         group, slots = send_idx.shape
-        columns, rounds, lists = exchange_plan(send_idx, src_idx, n_own)
+        columns, rounds, count, lists = exchange_plan(send_idx, src_idx, train_mask, n_own)
         n_recv = group * LANES
         starts = jnp.sum(dst_idx[None, :] < (jnp.arange(n_own // DST_TILE + 1) * DST_TILE)[:, None],
                          axis=1, dtype=jnp.int32)
@@ -283,11 +405,12 @@
         hidden_2 = jax.nn.relu(pre_2).astype(jnp.bfloat16)
         mean_3, logits = layer(hidden_2, w_self_3, w_neigh_3, bias_3)
         loss_sum, d_logits = head_grad(logits, labels, train_mask)
-        totals = lax.psum(jnp.stack([loss_sum, jnp.sum(train_mask)]), GROUP_AXIS)
-
-        d_pre_3 = d_logits / totals[1]
+
+        d_pre_3 = d_logits / count
         d_bf_3 = d_pre_3.astype(jnp.bfloat16)
-        g_self_3, g_neigh_3, g_bias_3 = weight_grads(hidden_2, mean_3, d_pre_3, d_bf_3)
+        g_self_3 = jnp.einsum('ne,nd->ed', d_bf_3, hidden_2, preferred_element_type=F32)
+        g_neigh_3 = jnp.einsum('ne,nd->ed', d_bf_3, mean_3, preferred_element_type=F32)
+        g_bias_3 = jnp.sum(d_pre_3, axis=0)
         d_self_3, d_mean_3 = input_grads(d_bf_3, w_self_3, w_neigh_3)
         d_pre_2 = jnp.where(pre_2 > 0, back_to_owners(d_mean_3, d_self_3), 0.0)
         d_bf_2 = d_pre_2.astype(jnp.bfloat16)
@@ -297,9 +420,18 @@
         d_bf_1 = d_pre_1.astype(jnp.bfloat16)
         g_self_1, g_neigh_1, g_bias_1 = weight_grads(features, mean_1, d_pre_1, d_bf_1)
 
-        grads = lax.psum((g_self_1, g_neigh_1, g_bias_1, g_self_2, g_neigh_2, g_bias_2,
-                          g_self_3, g_neigh_3, g_bias_3), GROUP_AXIS)
-        return (totals[0] / totals[1],) + tuple(grads)
+        classes = g_bias_3.shape[0]
+        small = jnp.concatenate([g_bias_1, g_bias_2, jnp.pad(g_bias_3, (0, LANES - classes)),
+                                 jnp.full((LANES,), loss_sum / count)]).reshape(-1, LANES)
+        small = jnp.pad(small, ((0, 8 - small.shape[0]), (0, 0)))
+        summed = add_up((g_self_1, g_neigh_1, g_self_2, g_neigh_2, g_self_3, g_neigh_3, small), group)
+        outs = unpack(summed, (g_self_1.shape, g_neigh_1.shape, g_self_2.shape, g_neigh_2.shape,
+                               w_self_3.shape, w_neigh_3.shape), (False,) * 4 + (True,) * 2)
+        gs_1, gn_1, gs_2, gn_2, gs_3, gn_3, small = outs
+        small = small.reshape(-1)
+        n_1, n_2 = g_bias_1.shape[0], g_bias_2.shape[0]
+        return (small[n_1 + n_2 + LANES], gs_1, gn_1, small[:n_1], gs_2, gn_2, small[n_1:n_1 + n_2],
+                gs_3, gn_3, small[n_1 + n_2:n_1 + n_2 + classes])
 
     sharded = P(GROUP_AXIS)
     whole = P()

time: 826 us -> 485 us (0.59)
  waiting for transfers between devices: 421 us -> 158 us
  blocking collectives: 38.2 us -> 0 us
  Pallas kernels: 193 us -> 175 us
  between operations: 20.4 us -> 6.35 us
    psum x2 -> x0, waiting for transfers between devices: 260 us -> none  [device_step(): lax.psum((g_self_1, g_neigh_1, g_bias_1, g_self_2, g_neigh_2, g_bias_2, g...]
    pallas_call x1, Pallas kernels: 100 us -> 50.1 us  [adjacency(): pl.pallas_call(functools.partial(adjacency_kernel, n_own), grid_spec=grid...]
    psum x1 -> x0, blocking collectives: 38.2 us -> none  [device_step(): totals = lax.psum(jnp.stack([loss_sum, jnp.sum(train_mask)]), GROUP_AXIS)]
    pallas_call x0 -> x2, Pallas kernels: none -> 31.7 us  [the longest x1 29.6 us: add_up(): pl.pallas_call(functools.partial(add_up_kernel, n_chips, rows), in_specs=...]
    unnamed x110 -> x99, local copies, waits for them, and re-layouts: 18.8 us -> 10.5 us
  transfers between devices with their start and end apart: 8 -> 6, of which waited for: 7 -> 5; matrix products, arithmetic and copies ran while one was open for 7% -> 11% of each run, Pallas kernels for 12% -> 11%
where the time goes in v2:
time: 485 us; the launch traced here: 476 us
  Pallas kernels  175 us (36%)
  waiting for transfers between devices  158 us (33%)
  matrix products  67.7 us (14%)
  starting transfers between devices  29.1 us (6%)
  other arithmetic  19.4 us (4%)
  local copies, waits for them, and re-layouts  16.8 us (3%)
  between operations  6.35 us (1%)
    all_to_all x5, waiting for transfers between devices, swap(): return lax.all_to_all(rows, GROUP_AXIS, 0, 0, tiled=True)  151 us
    pallas_call x1, Pallas kernels, adjacency(): pl.pallas_call(functools.partial(adjacency_kernel, n_own), grid_spec=grid...  50.1 us
    pallas_call x3, Pallas kernels, gather_in(): pl.pallas_call(gather_in_kernel, grid=(n_own // DST_TILE,), in_specs=[pl....  35.2 us
    pallas_call x1, Pallas kernels, add_up(): pl.pallas_call(functools.partial(add_up_kernel, n_chips, rows), in_specs=...  29.6 us
    pallas_call x2, Pallas kernels, spread_out(): pl.pallas_call(spread_out_kernel, grid=(n_recv // COLS,), in_specs=[pl.Bl...  23.7 us
    all_to_all x5, starting transfers between devices, swap(): return lax.all_to_all(rows, GROUP_AXIS, 0, 0, tiled=True)  21.5 us
    dot_general x3, matrix products, aggregate(): jnp.dot(adj_own, hidden, preferred_element_type=F32)  20.9 us
    pallas_call x3, Pallas kernels, pick(): pl.pallas_call(pick_kernel, grid=(group // BATCH,), in_specs=[pl.BlockSpe...  20 us
  transfers between devices with their start and end apart: 6, of which 5 were waited for; matrix products, arithmetic and copies ran while one was open for 11% of the time, Pallas kernels for 11%

profile of v2, /device:TPU:0, one launch (start us, length us, event | category | flops | bytes accessed | tf_op | source)
XLA Modules:
  0.0 476.0 jit_solution(11044871281121359371)
XLA Ops:
  2.2 2.3 fusion.10
  4.6 0.9 fusion.25
  10.1 3.5 fusion.16
  13.6 2.9 fusion.1
  17.1 7.6 %all-to-all-start.5 = ((s32[32,1,640]{2,1,0:T(1,128)}), s32[32,1,640]{2,1,0:T(1,128)S(1)}, u32[]{:S(2)}, u32[]{:S(2)}) async-start(s32[32,1,640]{2,1,0:T(1,128)} %copy.38), calls=%async_computation.5 | async-start | bytes 163840 | tf_op jit(solution)/shard_map/all_to_all | solution.py:328
  25.0 7.1 %all-to-all-done.5 = s32[32,1,640]{2,1,0:T(1,128)S(1)} async-done(((s32[32,1,640]{2,1,0:T(1,128)}), s32[32,1,640]{2,1,0:T(1,128)S(1)}, u32[]{:S(2)}, u32[]{:S(2)}) %all-to-all-start.5) | async-done | bytes 81952 | tf_op jit(solution)/shard_map/all_to_all | solution.py:328
  32.1 4.2 select_reduce_fusion
  36.9 6.6 %pick.6 = bf16[32,128,128]{2,1,0:T(8,128)(2,1)} custom-call(s32[32,128]{1,0:T(8,128)} %slice_bitcast_fusion.list_ref, bf16[2048,128]{1,0:T(8,128)(2,1)S(1)} %copy-done.25), custom_call_target="tpu_custom_call" | custom-call | flops 2147483648 | bytes 4000000 | tf_op jit(solution)/shard_map/pick/pallas_call | solution.py:111
  43.5 2.6 all-to-all-start.6
  46.2 50.1 %adjacency.6 = (bf16[2048,2048]{1,0:T(8,128)(2,1)}, bf16[2048,4096]{1,0:T(8,128)(2,1)}) custom-call(s32[9]{0:T(128)S(1)} %convert_reduce_fusion.starts, s32[1]{0:T(128)} %constant.125.clone.1.parts, s32[56,128]{1,0:T(8,128)} %get-tuple-element.405.dst_ref, s32[56,128]{1,0:T(8,128)} %get-tuple-element.404.col_ref), custom_call_target="tpu_custom_call" | custom-call | flops 30000001024 | bytes 40000000 | tf_op jit(solution)/shard_map/adjacency/pallas_call | solution.py:84
  96.2 1.8 fusion.44
  98.0 6.8 %fusion.45.add_ref = f32[2048,128]{1,0:T(8,128)} fusion(bf16[2048,2048]{1,0:T(8,128)(2,1)} %get-tuple-element.240, bf16[2048,128]{1,0:T(8,128)(2,1)S(1)} %copy-done.25), kind=kOutput, calls=%fused_computation.121 | convolution fusion | flops 1073741824 | bytes 9961472 | tf_op jit(solution)/shard_map/dot_general | solution.py:381
  105.5 1.0 copy-done.21
  106.5 10.7 %gather_in.6 = f32[2048,128]{1,0:T(8,128)S(1)} custom-call(bf16[2048,4096]{1,0:T(8,128)(2,1)} %get-tuple-element.239.adj_ref, bf16[4096,128]{1,0:T(8,128)(2,1)} %bitcast.159, f32[2048,128]{1,0:T(8,128)} %fusion.45.add_ref), custom_call_target="tpu_custom_call" | custom-call | flops 2147483648 | bytes 20000000 | tf_op jit(solution)/shard_map/gather_in/pallas_call | solution.py:161
  117.2 1.1 while.50
  118.4 3.8 maximum_convert_fusion.1
  122.2 6.7 %pick.7 = bf16[32,128,256]{2,1,0:T(8,128)(2,1)} custom-call(s32[32,128]{1,0:T(8,128)} %slice_bitcast_fusion.list_ref, bf16[2048,256]{1,0:T(8,128)(2,1)S(1)} %get-tuple-element.726.rows_ref), custom_call_target="tpu_custom_call" | custom-call | flops 4294967296 | bytes 4000000 | tf_op jit(solution)/shard_map/pick/pallas_call | solution.py:111
  128.9 5.8 %all-to-all-start.7 = ((bf16[32,128,256]{2,1,0:T(8,128)(2,1)}), bf16[32,128,256]{2,1,0:T(8,128)(2,1)S(1)}, u32[]{:S(2)}, u32[]{:S(2)}) async-start(bf16[32,128,256]{2,1,0:T(8,128)(2,1)} %pick.7), calls=%async_computation.7 | async-start | bytes 4194304 | tf_op jit(solution)/shard_map/all_to_all | solution.py:374
  134.7 1.8 fusion.46
  136.5 7.0 %fusion.47.add_ref = f32[2048,256]{1,0:T(8,128)} fusion(bf16[2048,2048]{1,0:T(8,128)(2,1)} %get-tuple-element.240, bf16[2048,256]{1,0:T(8,128)(2,1)S(1)} %get-tuple-element.726.rows_ref), kind=kOutput, calls=%fused_computation.123 | convolution fusion | flops 2147483648 | bytes 11534336 | tf_op jit(solution)/shard_map/dot_general | solution.py:381
  143.6 39.8 %all-to-all-done.7 = bf16[32,128,256]{2,1,0:T(8,128)(2,1)S(1)} async-done(((bf16[32,128,256]{2,1,0:T(8,128)(2,1)}), bf16[32,128,256]{2,1,0:T(8,128)(2,1)S(1)}, u32[]{:S(2)}, u32[]{:S(2)}) %all-to-all-start.7) | async-done | bytes 2097184 | tf_op jit(solution)/shard_map/all_to_all | solution.py:374
  183.4 1.4 copy-done.20
  184.8 12.3 %gather_in.7 = f32[2048,256]{1,0:T(8,128)} custom-call(bf16[2048,4096]{1,0:T(8,128)(2,1)} %get-tuple-element.239.adj_ref, bf16[4096,256]{1,0:T(8,128)(2,1)} %bitcast.158, f32[2048,256]{1,0:T(8,128)} %fusion.47.add_ref), custom_call_target="tpu_custom_call" | custom-call | flops 4294967296 | bytes 20000000 | tf_op jit(solution)/shard_map/gather_in/pallas_call | solution.py:161
  197.0 0.9 while.51
  197.9 1.0 copy-done.17
  198.9 4.1 maximum_convert_fusion
  203.0 6.7 %pick.8 = bf16[32,128,256]{2,1,0:T(8,128)(2,1)} custom-call(s32[32,128]{1,0:T(8,128)} %slice_bitcast_fusion.list_ref, bf16[2048,256]{1,0:T(8,128)(2,1)S(1)} %get-tuple-element.759.rows_ref), custom_call_target="tpu_custom_call" | custom-call | flops 4294967296 | bytes 4000000 | tf_op jit(solution)/shard_map/pick/pallas_call | solution.py:111
  209.7 4.2 all-to-all-start.8
  214.5 1.1 fusion.48
  215.7 7.1 %fusion.49.add_ref = f32[2048,256]{1,0:T(8,128)} fusion(bf16[2048,2048]{1,0:T(8,128)(2,1)} %get-tuple-element.240, bf16[2048,256]{1,0:T(8,128)(2,1)S(1)} %get-tuple-element.759.rows_ref), kind=kOutput, calls=%fused_computation.125 | convolution fusion | flops 2147483648 | bytes 11534336 | tf_op jit(solution)/shard_map/dot_general | solution.py:381
  222.8 39.8 %all-to-all-done.8 = bf16[32,128,256]{2,1,0:T(8,128)(2,1)S(1)} async-done(((bf16[32,128,256]{2,1,0:T(8,128)(2,1)}), bf16[32,128,256]{2,1,0:T(8,128)(2,1)S(1)}, u32[]{:S(2)}, u32[]{:S(2)}) %all-to-all-start.8) | async-done | bytes 2097184 | tf_op jit(solution)/shard_map/all_to_all | solution.py:374
  262.5 1.3 copy-done.19
  263.8 12.3 %gather_in.8 = f32[2048,256]{1,0:T(8,128)} custom-call(bf16[2048,4096]{1,0:T(8,128)(2,1)} %get-tuple-element.239.adj_ref, bf16[4096,256]{1,0:T(8,128)(2,1)} %bitcast.157, f32[2048,256]{1,0:T(8,128)} %fusion.49.add_ref), custom_call_target="tpu_custom_call" | custom-call | flops 4294967296 | bytes 20000000 | tf_op jit(solution)/shard_map/gather_in/pallas_call | solution.py:161
  276.9 2.5 fusion.43
  280.8 12.0 %spread_out.4 = bf16[4096,256]{1,0:T(8,128)(2,1)} custom-call(bf16[2048,4096]{1,0:T(8,128)(2,1)} %get-tuple-element.239.adj_ref, bf16[2048,256]{1,0:T(8,128)(2,1)S(1)} %fusion.8.rows_ref), custom_call_target="tpu_custom_call" | custom-call | flops 4294967296 | bytes 20000000 | tf_op jit(solution)/shard_map/spread_out/pallas_call | solution.py:182
  292.8 4.5 all-to-all-start.9
  297.3 6.0 %fusion.50 = f32[2048,256]{1,0:T(8,128)S(1)} fusion(bf16[2048,2048]{1,0:T(8,128)(2,1)} %get-tuple-element.240, bf16[2048,256]{1,0:T(8,128)(2,1)S(1)} %fusion.8.rows_ref), kind=kOutput, calls=%fused_computation.126 | convolution fusion | flops 2147483648 | bytes 11534336 | tf_op jit(solution)/shard_map/nt,nd->td/dot_general | solution.py:398
  303.4 1.8 convolution_add_fusion.add_ref
  305.2 40.9 %all-to-all-done.9.sent_ref = bf16[32,128,256]{2,1,0:T(8,128)(2,1)} async-done(((bf16[32,128,256]{2,1,0:T(8,128)(2,1)}), bf16[32,128,256]{2,1,0:T(8,128)(2,1)}, u32[]{:S(2)}, u32[]{:S(2)}) %all-to-all-start.9) | async-done | bytes 2097184 | tf_op jit(solution)/shard_map/all_to_all | solution.py:374
  346.1 7.0 %put_back.4 = f32[2048,256]{1,0:T(8,128)S(1)} custom-call(s32[32,128]{1,0:T(8,128)} %slice_bitcast_fusion.list_ref, bf16[32,128,256]{2,1,0:T(8,128)(2,1)} %all-to-all-done.9.sent_ref, f32[2048,256]{1,0:T(8,128)} %convolution_add_fusion.add_ref), custom_call_target="tpu_custom_call" | custom-call | flops 4294967296 | bytes 8000000 | tf_op jit(solution)/shard_map/put_back/pallas_call | solution.py:140
  353.8 2.7 fusion.14
  356.5 1.0 copy-done.12
  358.0 11.7 %spread_out.5 = bf16[4096,256]{1,0:T(8,128)(2,1)} custom-call(bf16[2048,4096]{1,0:T(8,128)(2,1)} %get-tuple-element.239.adj_ref, bf16[2048,256]{1,0:T(8,128)(2,1)S(1)} %fusion.7.rows_ref), custom_call_target="tpu_custom_call" | custom-call | flops 4294967296 | bytes 20000000 | tf_op jit(solution)/shard_map/spread_out/pallas_call | solution.py:182
  369.7 4.4 all-to-all-start.10
  375.3 2.3 fusion.53.refs_4_
  377.6 1.1 fusion.42.refs_5_
  378.7 2.6 fusion.13
  381.3 1.2 fusion.52.refs_2_
  383.0 1.6 fusion.41.refs_3_
  384.6 6.0 %fusion.51 = f32[2048,256]{1,0:T(8,128)S(1)} fusion(bf16[2048,2048]{1,0:T(8,128)(2,1)} %get-tuple-element.240, bf16[2048,256]{1,0:T(8,128)(2,1)S(1)} %fusion.7.rows_ref), kind=kOutput, calls=%fused_computation.127 | convolution fusion | flops 2147483648 | bytes 11534336 | tf_op jit(solution)/shard_map/nt,nd->td/dot_general | solution.py:398
  390.6 1.8 convolution_add_fusion.1.add_ref
  392.4 30.4 %all-to-all-done.10.sent_ref = bf16[32,128,256]{2,1,0:T(8,128)(2,1)} async-done(((bf16[32,128,256]{2,1,0:T(8,128)(2,1)}), bf16[32,128,256]{2,1,0:T(8,128)(2,1)}, u32[]{:S(2)}, u32[]{:S(2)}) %all-to-all-start.10) | async-done | bytes 2097184 | tf_op jit(solution)/shard_map/all_to_all | solution.py:374
  422.7 7.0 %put_back.5 = f32[2048,256]{1,0:T(8,128)S(1)} custom-call(s32[32,128]{1,0:T(8,128)} %slice_bitcast_fusion.list_ref, bf16[32,128,256]{2,1,0:T(8,128)(2,1)} %all-to-all-done.10.sent_ref, f32[2048,256]{1,0:T(8,128)} %convolution_add_fusion.1.add_ref), custom_call_target="tpu_custom_call" | custom-call | flops 4294967296 | bytes 8000000 | tf_op jit(solution)/shard_map/put_back/pallas_call | solution.py:140
  430.5 2.1 fusion.11
  433.1 0.8 copy-done.9
  433.9 1.4 fusion.40.refs_1_
  435.3 1.0 convolution_bitcast_fusion.refs_0_
  436.9 29.6 %add_up.1.packed_ref = f32[1792,128]{1,0:T(8,128)} custom-call(f32[128,256]{1,0:T(8,128)} %convolution_bitcast_fusion.refs_0_, f32[128,256]{1,0:T(8,128)} %fusion.40.refs_1_, f32[256,256]{1,0:T(8,128)} %fusion.52.refs_2_, f32[256,256]{1,0:T(8,128)} %fusion.41.refs_3_, f32[40,256]{1,0:T(8,128)} %fusion.53.refs_4_, f32[40,256]{1,0:T(8,128)} %fusion.42.refs_5_, ...), custom_call_target="tpu_custom_call" | custom-call | tf_op jit(solution)/shard_map/add_up/pallas_call | solution.py:260
  466.5 2.2 unpack.1
  468.6 1.2 slice.46
  469.8 1.2 slice.51
  471.0 1.3 slice_bitcast_fusion.1
  472.4 1.6 copy.41
  474.0 1.6 copy.42
  (121 shorter events, 11.4 us)
Async XLA Ops:
  0.6 198.2 %copy-start = (bf16[256,256]{1,0:T(8,128)(2,1)S(1)}, bf16[256,256]{1,0:T(8,128)(2,1)}, u32[]{:S(2)}) copy-start(bf16[256,256]{1,0:T(8,128)(2,1)} %param.37) | copy-start | bytes 393220
  2.2 4.5 copy-start.38
  2.2 5.8 %copy-start.42 = (s32[32,512]{1,0:T(8,128)S(1)}, s32[32,512]{1,0:T(8,128)}, u32[]{:S(2)}) copy-start(s32[32,512]{1,0:T(8,128)} %param.29) | copy-start | bytes 196612
  13.6 2.9 copy-start.34
  13.6 2.9 copy-start.15
  13.6 23.3 %copy-start.25 = (bf16[2048,128]{1,0:T(8,128)(2,1)S(1)}, bf16[2048,128]{1,0:T(8,128)(2,1)}, u32[]{:S(2)}) copy-start(bf16[2048,128]{1,0:T(8,128)(2,1)} %rows_ref.1) | copy-start | bytes 1572868
  17.1 14.9 %all-to-all-start.5 = ((s32[32,1,640]{2,1,0:T(1,128)}), s32[32,1,640]{2,1,0:T(1,128)S(1)}, u32[]{:S(2)}, u32[]{:S(2)}) async-start(s32[32,1,640]{2,1,0:T(1,128)} %copy.38), calls=%async_computation.5 | async-start | bytes 163840 | tf_op jit(solution)/shard_map/all_to_all | solution.py:328
  43.5 62.0 %all-to-all-start.6 = ((bf16[32,128,128]{2,1,0:T(8,128)(2,1)}), bf16[32,128,128]{2,1,0:T(8,128)(2,1)S(1)}, u32[]{:S(2)}, u32[]{:S(2)}) async-start(bf16[32,128,128]{2,1,0:T(8,128)(2,1)} %pick.6), calls=%async_computation.6 | async-start | bytes 2097152 | tf_op jit(solution)/shard_map/all_to_all | solution.py:374
  46.2 50.1 %copy-start.43 = (bf16[128,256]{1,0:T(8,128)(2,1)S(1)}, bf16[128,256]{1,0:T(8,128)(2,1)}, u32[]{:S(2)}) copy-start(bf16[128,256]{1,0:T(8,128)(2,1)} %param.33) | copy-start | bytes 196612
  105.5 1.0 copy-start.21
  117.2 1.1 copy-start.27
  117.2 1.1 copy-start.41
  117.2 1.1 copy-start.49
  118.3 3.8 copy-start.8
  128.9 5.8 %copy-start.32 = (bf16[256,256]{1,0:T(8,128)(2,1)S(1)}, bf16[256,256]{1,0:T(8,128)(2,1)}, u32[]{:S(2)}) copy-start(bf16[256,256]{1,0:T(8,128)(2,1)} %param.36) | copy-start | bytes 393220
  128.9 54.5 %all-to-all-start.7 = ((bf16[32,128,256]{2,1,0:T(8,128)(2,1)}), bf16[32,128,256]{2,1,0:T(8,128)(2,1)S(1)}, u32[]{:S(2)}, u32[]{:S(2)}) async-start(bf16[32,128,256]{2,1,0:T(8,128)(2,1)} %pick.7), calls=%async_computation.7 | async-start | bytes 4194304 | tf_op jit(solution)/shard_map/all_to_all | solution.py:374
  183.4 1.4 copy-start.20
  197.0 1.8 copy-start.28
  197.0 1.8 copy-start.48
  197.9 1.0 copy-start.17
  209.7 4.8 %copy-start.36 = (bf16[256,40]{0,1:T(8,128)(2,1)S(1)}, bf16[256,40]{0,1:T(8,128)(2,1)}, u32[]{:S(2)}) copy-start(bf16[256,40]{0,1:T(8,128)(2,1)} %param.39) | copy-start | bytes 61444
  209.7 52.8 %all-to-all-start.8 = ((bf16[32,128,256]{2,1,0:T(8,128)(2,1)}), bf16[32,128,256]{2,1,0:T(8,128)(2,1)S(1)}, u32[]{:S(2)}, u32[]{:S(2)}) async-start(bf16[32,128,256]{2,1,0:T(8,128)(2,1)} %pick.8), calls=%async_computation.8 | async-start | bytes 4194304 | tf_op jit(solution)/shard_map/all_to_all | solution.py:374
  262.5 1.3 copy-start.19
  276.1 0.7 copy-start.29
  276.1 0.8 copy-start.35
  276.1 0.8 copy-start.50
  276.8 3.9 copy-start.16
  276.8 2.6 copy-start.39
  276.8 2.6 copy-start.45
  280.2 23.1 %copy-start.22 = (bf16[2048,40]{0,1:T(8,128)(2,1)}, bf16[2048,40]{0,1:T(8,128)(2,1)S(1)}, u32[]{:S(2)}) copy-start(bf16[2048,40]{0,1:T(8,128)(2,1)S(1)} %get-tuple-element.387) | copy-start | bytes 491524
  280.8 16.6 %copy-start.10 = (bf16[2048,256]{1,0:T(8,128)(2,1)}, bf16[2048,256]{1,0:T(8,128)(2,1)S(1)}, u32[]{:S(2)}) copy-start(bf16[2048,256]{1,0:T(8,128)(2,1)S(1)} %fusion.8.rows_ref) | copy-start | bytes 3145732
  292.8 53.2 %all-to-all-start.9 = ((bf16[32,128,256]{2,1,0:T(8,128)(2,1)}), bf16[32,128,256]{2,1,0:T(8,128)(2,1)}, u32[]{:S(2)}, u32[]{:S(2)}) async-start(bf16[32,128,256]{2,1,0:T(8,128)(2,1)} %bitcast.156), calls=%async_computation.9 | async-start | bytes 4194304 | tf_op jit(solution)/shard_map/all_to_all | solution.py:374
  297.3 6.0 %copy-start.37 = (bf16[256,40]{0,1:T(8,128)(2,1)S(1)}, bf16[256,40]{0,1:T(8,128)(2,1)}, u32[]{:S(2)}) copy-start(bf16[256,40]{0,1:T(8,128)(2,1)} %param.39) | copy-start | bytes 61444
  305.2 47.9 %copy-start.11 = (bf16[2048,256]{1,0:T(8,128)(2,1)S(1)}, bf16[2048,256]{1,0:T(8,128)(2,1)}, u32[]{:S(2)}) copy-start(bf16[2048,256]{1,0:T(8,128)(2,1)} %copy-done.10) | copy-start | bytes 3145732
  353.8 2.7 copy-start.6
  353.8 2.7 copy-start.24
  353.8 3.7 copy-start.30
  356.5 1.0 copy-start.12
  369.6 4.4 copy-start.40
  369.6 4.4 copy-start.44
  369.7 5.7 %copy-start.23 = (bf16[2048,40]{0,1:T(8,128)(2,1)S(1)}, bf16[2048,40]{0,1:T(8,128)(2,1)}, u32[]{:S(2)}) copy-start(bf16[2048,40]{0,1:T(8,128)(2,1)} %copy-done.22) | copy-start | bytes 491524
  369.7 7.9 %copy-start.4 = (f32[2048,256]{1,0:T(8,128)S(1)}, f32[2048,256]{1,0:T(8,128)}, u32[]{:S(2)}) copy-start(f32[2048,256]{1,0:T(8,128)} %get-tuple-element.243) | copy-start | bytes 6291460
  369.7 53.1 %all-to-all-start.10 = ((bf16[32,128,256]{2,1,0:T(8,128)(2,1)}), bf16[32,128,256]{2,1,0:T(8,128)(2,1)}, u32[]{:S(2)}, u32[]{:S(2)}) async-start(bf16[32,128,256]{2,1,0:T(8,128)(2,1)} %bitcast.155), calls=%async_computation.10 | async-start | bytes 4194304 | tf_op jit(solution)/shard_map/all_to_all | solution.py:374
  375.3 3.4 copy-start.7
  378.7 2.6 copy-start.13
  378.7 2.6 copy-start.18
  381.3 1.7 copy-start.3
  384.6 6.0 %copy-start.33 = (bf16[256,256]{1,0:T(8,128)(2,1)S(1)}, bf16[256,256]{1,0:T(8,128)(2,1)}, u32[]{:S(2)}) copy-start(bf16[256,256]{1,0:T(8,128)(2,1)} %param.36) | copy-start | bytes 393220
  430.5 2.2 copy-start.14
  432.7 1.2 copy-start.9
  432.7 1.2 copy-start.31
  433.9 1.4 copy-start.26
  433.9 2.4 copy-start.46
  433.9 2.4 copy-start.47

commit v3 on v2

--- a/solution.py
+++ b/solution.py
@@ -13,6 +13,8 @@
 WINDOW = 8
 COLS = 512
 BATCH = 8
+PLANE = 8
+ROWS = 512
 VMEM_BYTES = 60 * 1024 * 1024
 MESH = pl.DeviceIdType.MESH
 F32 = jnp.float32
@@ -189,6 +191,177 @@
         cost_estimate=pl.CostEstimate(flops=2 * n_own * n_recv * width, bytes_accessed=20 * 10**6, transcendentals=0),
         name='spread_out',
     )(adj_rec, rows)
+
+
+def plane_order(me, planes):
+    z = lax.div(me, PLANE)
+    if planes == 4:
+        return [lax.rem(z + 2, 4), 3 - z, z + 1 - 2 * lax.rem(z, 2), z]
+    return [lax.rem(z + step, planes) for step in range(1, planes + 1)]
+
+
+def meet_all(barrier, me, group):
+    def signal(step, carry):
+        pl.semaphore_signal(barrier, inc=1, device_id=(lax.rem(me + step, group),), device_id_type=MESH)
+        return carry
+
+    lax.fori_loop(1, group, signal, 0)
+
+
+class Swap:
+    def __init__(self, me, outbox, inbox, send, recv):
+        self.me, self.outbox, self.inbox, self.send, self.recv = me, outbox, inbox, send, recv
+
+    def copy(self, peer, slot):
+        return pltpu.make_async_remote_copy(
+            src_ref=self.outbox.at[peer], dst_ref=self.inbox.at[slot], send_sem=self.send.at[peer],
+            recv_sem=self.recv.at[slot], device_id=(peer,), device_id_type=MESH)
+
+    def others(self, plane, own):
+        if own:
+            return [plane * PLANE + lax.rem(self.me + step, PLANE) for step in range(1, PLANE)]
+        return [plane * PLANE + step for step in range(PLANE)]
+
+    def send_plane(self, plane, own):
+        for peer in self.others(plane, own):
+            self.copy(peer, self.me).start()
+        if own:
+            self.inbox[self.me] = self.outbox[self.me]
+
+    def receive_plane(self, plane, own):
+        for peer in self.others(plane, own):
+            self.copy(peer, peer).wait_recv()
+        block = self.inbox[pl.ds(plane * PLANE, PLANE)]
+        return block.reshape(block.shape[0] * block.shape[1], block.shape[2])
+
+    def finish(self, planes):
+        for k, plane in enumerate(planes):
+            for peer in self.others(plane, k == len(planes) - 1):
+                self.copy(peer, self.me).wait_send()
+
+
+def fetch_adjacency(own_hbm, rec_hbm, own_ref, rec_ref, planes, sems):
+    span = rec_ref.shape[2]
+    own = pltpu.make_async_copy(own_hbm, own_ref, sems.at[len(planes)])
+    recs = [pltpu.make_async_copy(rec_hbm.at[:, pl.ds(pl.multiple_of(plane * span, span), span)], rec_ref.at[k],
+                                  sems.at[k]) for k, plane in enumerate(planes)]
+    return own, recs
+
+
+def exchange_in_kernel(group, list_ref, rows_ref, own_hbm, rec_hbm, out_ref,
+                       outbox, inbox, own_ref, rec_ref, send, recv, sems):
+    me = lax.axis_index(GROUP_AXIS)
+    planes = plane_order(me, group // PLANE)
+    barrier = pltpu.get_barrier_semaphore()
+    meet_all(barrier, me, group)
+    own_copy, rec_copies = fetch_adjacency(own_hbm, rec_hbm, own_ref, rec_ref, planes, sems)
+    for item in [own_copy] + rec_copies[::-1]:
+        item.start()
+    swap = Swap(me, outbox, inbox, send, recv)
+    n_rows = rows_ref.shape[0]
+    lanes = lax.broadcasted_iota(jnp.int32, (LANES, LANES), 1).astype(IDX)
+    met = False
+    for k, plane in enumerate(planes):
+        def pick_one(b, carry):
+            columns = as_columns(list_ref[pl.ds(plane * PLANE + b, 1), :]).astype(IDX)
+            hot = jnp.concatenate([jnp.where(columns == lanes + IDX(j * LANES), BF16(1), BF16(0))
+                                   for j in range(n_rows // LANES)], axis=1)
+            return hot
+
+        hot = jnp.concatenate([pick_one(b, 0) for b in range(PLANE)], axis=0)
+        picked = jnp.dot(hot, rows_ref[...], preferred_element_type=F32).astype(BF16)
+        outbox[pl.ds(plane * PLANE, PLANE)] = picked.reshape(PLANE, LANES, picked.shape[1])
+        if not met:
+            pl.semaphore_wait(barrier, group - 1)
+            met = True
+        swap.send_plane(plane, k == len(planes) - 1)
+    own_copy.wait()
+
+    def own_step(i, carry):
+        at = pl.ds(pl.multiple_of(i * ROWS, ROWS), ROWS)
+        out_ref[at, :] = jnp.dot(own_ref[at, :], rows_ref[...], preferred_element_type=F32)
+        return carry
+
+    lax.fori_loop(0, n_rows // ROWS, own_step, 0)
+    for k in [3, 2, 0, 1] if len(planes) == 4 else range(len(planes))[::-1]:
+        rec_copies[k].wait()
+        block = swap.receive_plane(planes[k], k == len(planes) - 1)
+
+        def rec_step(i, carry):
+            at = pl.ds(pl.multiple_of(i * ROWS, ROWS), ROWS)
+            out_ref[at, :] += jnp.dot(rec_ref[k, at, :], block, preferred_element_type=F32)
+            return carry
+
+        lax.fori_loop(0, n_rows // ROWS, rec_step, 0)
+    swap.finish(planes)
+
+
+def exchange_back_kernel(group, list_ref, grad_ref, add_ref, own_hbm, rec_hbm, out_ref,
+                         outbox, inbox, own_ref, rec_ref, send, recv, sems):
+    me = lax.axis_index(GROUP_AXIS)
+    planes = plane_order(me, group // PLANE)
+    barrier = pltpu.get_barrier_semaphore()
+    meet_all(barrier, me, group)
+    own_copy, rec_copies = fetch_adjacency(own_hbm, rec_hbm, own_ref, rec_ref, planes, sems)
+    for item in rec_copies + [own_copy]:
+        item.start()
+    swap = Swap(me, outbox, inbox, send, recv)
+    n_rows, width = grad_ref.shape
+    met = False
+    for k, plane in enumerate(planes):
+        rec_copies[k].wait()
+        part = lax.dot_general(rec_ref[k], grad_ref[...], (((0,), (0,)), ((), ())), preferred_element_type=F32)
+        outbox[pl.ds(plane * PLANE, PLANE)] = part.astype(BF16).reshape(PLANE, LANES, width)
+        if not met:
+            pl.semaphore_wait(barrier, group - 1)
+            met = True
+        swap.send_plane(plane, k == len(planes) - 1)
+    own_copy.wait()
+
+    def own_step(i, carry):
+        at = pl.ds(pl.multiple_of(i * ROWS, ROWS), ROWS)
+        out_ref[at, :] = add_ref[at, :] + lax.dot_general(
+            own_ref[:, at], grad_ref[...], (((0,), (0,)), ((), ())), preferred_element_type=F32)
+        return carry
+
+    lax.fori_loop(0, n_rows // ROWS, own_step, 0)
+    row_iota = lax.broadcasted_iota(jnp.int32, (ROWS, LANES), 0)
+    for k in [3, 2, 0, 1] if len(planes) == 4 else range(len(planes))[::-1]:
+        block = swap.receive_plane(planes[k], k == len(planes) - 1)
+        names = list_ref[pl.ds(pl.multiple_of(planes[k] * PLANE, PLANE), PLANE), :]
+
+        def rec_step(i, carry):
+            at = pl.ds(pl.multiple_of(i * ROWS, ROWS), ROWS)
+            rows = (row_iota + i * ROWS).astype(IDX)
+            hot = jnp.concatenate(
+                [jnp.where(rows == jnp.broadcast_to(names[b:b + 1, :], (ROWS, LANES)).astype(IDX), BF16(1), BF16(0))
+                 for b in range(PLANE)], axis=1)
+            out_ref[at, :] += jnp.dot(hot, block, preferred_element_type=F32)
+            return carry
+
+        lax.fori_loop(0, n_rows // ROWS, rec_step, 0)
+    swap.finish(planes)
+
+
+def exchange(body, which, name, lists, arrays, adj_own, adj_rec):
+    group = lists.shape[0]
+    n_rows, width = arrays[0].shape
+    planes = group // PLANE
+    vmem, anywhere = pl.BlockSpec(memory_space=pltpu.VMEM), pl.BlockSpec(memory_space=pl.ANY)
+    box = pltpu.VMEM((group, LANES, width), BF16)
+    return pl.pallas_call(
+        functools.partial(body, group),
+        in_specs=[vmem] * (1 + len(arrays)) + [anywhere] * 2, out_specs=vmem,
+        out_shape=jax.ShapeDtypeStruct((n_rows, width), F32),
+        scratch_shapes=[box, box, pltpu.VMEM(adj_own.shape, BF16),
+                        pltpu.VMEM((planes, n_rows, adj_rec.shape[1] // planes), BF16),
+                        pltpu.SemaphoreType.DMA((group,)), pltpu.SemaphoreType.DMA((group,)),
+                        pltpu.SemaphoreType.DMA((planes + 1,))],
+        compiler_params=pltpu.CompilerParams(collective_id=which, has_side_effects=True, vmem_limit_bytes=VMEM_BYTES),
+        cost_estimate=pl.CostEstimate(flops=2 * 2 * n_rows * adj_rec.shape[1] * width, bytes_accessed=30 * 10**6,
+                                      transcendentals=0),
+        name=name,
+    )(lists, *arrays, adj_own, adj_rec)
 
 
 def add_up_kernel(n_chips, rows, *refs):
@@ -373,37 +546,37 @@
         def swap(rows):
             return lax.all_to_all(rows, GROUP_AXIS, 0, 0, tiled=True)
 
-        def aggregate(hidden):
-            def one_round(part, adj_rec, total):
+        def aggregate(hidden, which):
+            def more(part, total):
                 received = swap(pick(lists[part], hidden))
-                return gather_in(adj_rec, received.reshape(n_recv, -1), total)
-
-            summed = one_round(0, adj_first, jnp.dot(adj_own, hidden, preferred_element_type=F32))
-            summed = lax.fori_loop(1, rounds, lambda part, total: one_round(part, adjacency_of(part)[1], total), summed)
+                return gather_in(adjacency_of(part)[1], received.reshape(n_recv, -1), total)
+
+            summed = exchange(exchange_in_kernel, which, 'exchange_in', lists[0], (hidden,), adj_own, adj_first)
+            summed = lax.fori_loop(1, rounds, more, summed)
             return (summed * inv_deg[:, None]).astype(BF16)
 
-        def layer(hidden, w_self, w_neigh, bias):
-            neigh_mean = aggregate(hidden)
+        def layer(hidden, w_self, w_neigh, bias, which):
+            neigh_mean = aggregate(hidden, which)
             pre_act = (jnp.dot(hidden, w_self, preferred_element_type=jnp.float32)
                        + jnp.dot(neigh_mean, w_neigh, preferred_element_type=jnp.float32) + bias)
             return neigh_mean, pre_act
 
-        def back_to_owners(d_mean, d_self):
+        def back_to_owners(d_mean, d_self, which):
             d_sum = (d_mean * inv_deg[:, None]).astype(BF16)
 
-            def one_round(part, adj_rec, total):
-                returned = swap(spread_out(adj_rec, d_sum).reshape(group, LANES, -1))
+            def more(part, total):
+                returned = swap(spread_out(adjacency_of(part)[1], d_sum).reshape(group, LANES, -1))
                 return put_back(lists[part], returned, total)
 
-            d_own = d_self + jnp.einsum('nt,nd->td', adj_own, d_sum, preferred_element_type=F32)
-            return lax.fori_loop(1, rounds, lambda part, total: one_round(part, adjacency_of(part)[1], total),
-                                 one_round(0, adj_first, d_own))
-
-        mean_1, pre_1 = layer(features, w_self_1, w_neigh_1, bias_1)
+            d_hidden = exchange(exchange_back_kernel, which, 'exchange_back', lists[0], (d_sum, d_self),
+                                adj_own, adj_first)
+            return lax.fori_loop(1, rounds, more, d_hidden)
+
+        mean_1, pre_1 = layer(features, w_self_1, w_neigh_1, bias_1, 1)
         hidden_1 = jax.nn.relu(pre_1).astype(jnp.bfloat16)
-        mean_2, pre_2 = layer(hidden_1, w_self_2, w_neigh_2, bias_2)
+        mean_2, pre_2 = layer(hidden_1, w_self_2, w_neigh_2, bias_2, 2)
         hidden_2 = jax.nn.relu(pre_2).astype(jnp.bfloat16)
-        mean_3, logits = layer(hidden_2, w_self_3, w_neigh_3, bias_3)
+        mean_3, logits = layer(hidden_2, w_self_3, w_neigh_3, bias_3, 3)
         loss_sum, d_logits = head_grad(logits, labels, train_mask)
 
         d_pre_3 = d_logits / count
@@ -412,11 +585,11 @@
         g_neigh_3 = jnp.einsum('ne,nd->ed', d_bf_3, mean_3, preferred_element_type=F32)
         g_bias_3 = jnp.sum(d_pre_3, axis=0)
         d_self_3, d_mean_3 = input_grads(d_bf_3, w_self_3, w_neigh_3)
-        d_pre_2 = jnp.where(pre_2 > 0, back_to_owners(d_mean_3, d_self_3), 0.0)
+        d_pre_2 = jnp.where(pre_2 > 0, back_to_owners(d_mean_3, d_self_3, 4), 0.0)
         d_bf_2 = d_pre_2.astype(jnp.bfloat16)
         g_self_2, g_neigh_2, g_bias_2 = weight_grads(hidden_1, mean_2, d_pre_2, d_bf_2)
         d_self_2, d_mean_2 = input_grads(d_bf_2, w_self_2, w_neigh_2)
-        d_pre_1 = jnp.where(pre_1 > 0, back_to_owners(d_mean_2, d_self_2), 0.0)
+        d_pre_1 = jnp.where(pre_1 > 0, back_to_owners(d_mean_2, d_self_2, 5), 0.0)
         d_bf_1 = d_pre_1.astype(jnp.bfloat16)
         g_self_1, g_neigh_1, g_bias_1 = weight_grads(features, mean_1, d_pre_1, d_bf_1)
 

time: 485 us -> 451 us (0.930)
  the two profiles are of different devices: /device:TPU:0 before, /device:TPU:29 now
where the time goes in v3:
time: 451 us; the launch traced here: 443 us
  Pallas kernels  359 us (80%)
  matrix products  33.2 us (7%)
  other arithmetic  17.1 us (4%)
  local copies, waits for them, and re-layouts  12.7 us (3%)
  starting transfers between devices  6.42 us (1%)
  between operations  6.21 us (1%)
  loops' own time  4.61 us (1%)
    pallas_call x5, Pallas kernels, exchange(): pl.pallas_call(functools.partial(body, group), in_specs=[vmem] * (1 + len...  262 us
    pallas_call x1, Pallas kernels, adjacency(): pl.pallas_call(functools.partial(adjacency_kernel, n_own), grid_spec=grid...  50.2 us
    pallas_call x1, Pallas kernels, add_up(): pl.pallas_call(functools.partial(add_up_kernel, n_chips, rows), in_specs=...  44.7 us
    dot_general x3, matrix products, layer(): jnp.dot(neigh_mean, w_neigh, preferred_element_type=jnp.float32)  10.1 us
  transfers between devices with their start and end apart: 1, of which 1 were waited for; matrix products, arithmetic and copies ran while one was open for 0% of the time, Pallas kernels for 0%

profile of v3, /device:TPU:29, one launch (start us, length us, event | category | flops | bytes accessed | tf_op | source)
XLA Modules:
  0.0 443.3 jit_solution(7101783340685773050)
XLA Ops:
  0.6 0.0 copy-start
  0.7 0.8 add_compare_fusion.1
  1.4 0.8 add_select_fusion.3
  2.2 2.3 fusion.10
  4.6 0.9 fusion.25
  6.7 0.6 reduce_sum.100
  9.4 0.7 copy.38
  10.1 3.5 fusion.16
  13.6 0.0 copy-start.13
  13.6 0.0 copy-start.31
  13.6 2.9 fusion.1
  16.5 0.2 convert_reduce_fusion.starts
  16.7 0.6 pad_bitcast_fusion.10
  17.4 1.8 fusion.44
  19.1 50.2 %adjacency.6 = (bf16[2048,2048]{1,0:T(8,128)(2,1)}, bf16[2048,4096]{1,0:T(8,128)(2,1)}) custom-call(s32[9]{0:T(128)S(1)} %convert_reduce_fusion.starts, s32[1]{0:T(128)} %constant.134.clone.1.parts, s32[56,128]{1,0:T(8,128)} %get-tuple-element.405.dst_ref, s32[56,128]{1,0:T(8,128)} %get-tuple-element.404.col_ref), custom_call_target="tpu_custom_call" | custom-call | flops 30000001024 | bytes 40000000 | tf_op jit(solution)/shard_map/adjacency/pallas_call | solution.py:86
  69.3 6.4 %all-to-all-start.5 = ((s32[32,1,640]{2,1,0:T(1,128)}), s32[32,1,640]{2,1,0:T(1,128)S(1)}, u32[]{:S(2)}, u32[]{:S(2)}) async-start(s32[32,1,640]{2,1,0:T(1,128)} %copy.38), calls=%async_computation.5 | async-start | bytes 163840 | tf_op jit(solution)/shard_map/all_to_all | solution.py:501
  75.8 3.7 all-to-all-done.5
  79.4 0.7 slice_reduce_fusion.1
  80.8 4.2 select_reduce_fusion
  85.0 0.6 slice_bitcast_fusion.list_ref
  85.6 32.7 %exchange_in.3 = f32[2048,128]{1,0:T(8,128)S(1)} custom-call(s32[32,128]{1,0:T(8,128)} %slice_bitcast_fusion.list_ref, bf16[2048,128]{1,0:T(8,128)(2,1)S(1)} %copy-done.13, bf16[2048,2048]{1,0:T(8,128)(2,1)} %get-tuple-element.239.own_hbm, bf16[2048,4096]{1,0:T(8,128)(2,1)} %get-tuple-element.240.rec_hbm), custom_call_target="tpu_custom_call" | custom-call | flops 4294967296 | bytes 30000000 | tf_op jit(solution)/shard_map/exchange_in/pallas_call | solution.py:352
  118.3 0.9 while.50
  119.3 3.8 maximum_convert_fusion.1
  123.1 48.7 %exchange_in.4 = f32[2048,256]{1,0:T(8,128)} custom-call(s32[32,128]{1,0:T(8,128)} %slice_bitcast_fusion.list_ref, bf16[2048,256]{1,0:T(8,128)(2,1)S(1)} %get-tuple-element.726.rows_ref, bf16[2048,2048]{1,0:T(8,128)(2,1)} %get-tuple-element.239.own_hbm, bf16[2048,4096]{1,0:T(8,128)(2,1)} %get-tuple-element.240.rec_hbm), custom_call_target="tpu_custom_call" | custom-call | flops 8589934592 | bytes 30000000 | tf_op jit(solution)/shard_map/exchange_in/pallas_call | solution.py:352
  171.8 1.7 fusion.45
  173.5 1.1 while.51
  174.6 1.0 copy-done.11
  175.6 4.1 maximum_convert_fusion
  179.7 61.0 %exchange_in.5 = f32[2048,256]{1,0:T(8,128)} custom-call(s32[32,128]{1,0:T(8,128)} %slice_bitcast_fusion.list_ref, bf16[2048,256]{1,0:T(8,128)(2,1)S(1)} %get-tuple-element.759.rows_ref, bf16[2048,2048]{1,0:T(8,128)(2,1)} %get-tuple-element.239.own_hbm, bf16[2048,4096]{1,0:T(8,128)(2,1)} %get-tuple-element.240.rec_hbm), custom_call_target="tpu_custom_call" | custom-call | flops 8589934592 | bytes 30000000 | tf_op jit(solution)/shard_map/exchange_in/pallas_call | solution.py:352
  240.8 1.2 fusion.46
  241.9 0.9 while.52
  242.9 2.3 fusion.43
  245.1 0.1 exponential_reduce_fusion
  245.2 0.8 select_reduce_fusion.1
  246.0 1.1 fusion.42.refs_5_
  247.1 0.9 fusion.50.refs_4_
  248.0 0.5 fusion.8.grad_ref
  248.5 1.8 fusion.47.add_ref
  250.3 61.0 %exchange_back.2 = f32[2048,256]{1,0:T(8,128)S(1)} custom-call(s32[32,128]{1,0:T(8,128)} %slice_bitcast_fusion.list_ref, bf16[2048,256]{1,0:T(8,128)(2,1)S(1)} %fusion.8.grad_ref, f32[2048,256]{1,0:T(8,128)} %fusion.47.add_ref, bf16[2048,2048]{1,0:T(8,128)(2,1)} %get-tuple-element.239.own_hbm, bf16[2048,4096]{1,0:T(8,128)(2,1)} %get-tuple-element.240.rec_hbm), custom_call_target="tpu_custom_call" | custom-call | flops 8589934592 | bytes 30000000 | tf_op jit(solution)/shard_map/exchange_back/pallas_call | solution.py:352
  311.4 0.9 while.53
  312.2 2.6 fusion.13
  314.9 0.4 fusion.14
  315.3 1.2 copy-done.5
  316.5 1.6 fusion.41.refs_3_
  318.0 1.2 fusion.49.refs_2_
  319.2 0.5 fusion.7.grad_ref
  319.7 1.8 fusion.48.add_ref
  321.5 58.9 %exchange_back.3 = f32[2048,256]{1,0:T(8,128)S(1)} custom-call(s32[32,128]{1,0:T(8,128)} %slice_bitcast_fusion.list_ref, bf16[2048,256]{1,0:T(8,128)(2,1)S(1)} %fusion.7.grad_ref, f32[2048,256]{1,0:T(8,128)} %fusion.48.add_ref, bf16[2048,2048]{1,0:T(8,128)(2,1)} %get-tuple-element.239.own_hbm, bf16[2048,4096]{1,0:T(8,128)(2,1)} %get-tuple-element.240.rec_hbm), custom_call_target="tpu_custom_call" | custom-call | flops 8589934592 | bytes 30000000 | tf_op jit(solution)/shard_map/exchange_back/pallas_call | solution.py:352
  380.4 0.9 while.54
  381.4 2.1 fusion.11
  383.4 0.2 copy-done.9
  383.6 0.4 fusion.12
  384.0 0.8 copy-done.7
  384.8 1.4 fusion.40.refs_1_
  386.2 1.0 convolution_bitcast_fusion.refs_0_
  387.2 0.6 multiply_reduce_fusion
  388.5 0.6 pad.21.refs_6_
  389.1 44.7 %add_up.1.packed_ref = f32[1792,128]{1,0:T(8,128)} custom-call(f32[128,256]{1,0:T(8,128)} %convolution_bitcast_fusion.refs_0_, f32[128,256]{1,0:T(8,128)} %fusion.40.refs_1_, f32[256,256]{1,0:T(8,128)} %fusion.49.refs_2_, f32[256,256]{1,0:T(8,128)} %fusion.41.refs_3_, f32[40,256]{1,0:T(8,128)} %fusion.50.refs_4_, f32[40,256]{1,0:T(8,128)} %fusion.42.refs_5_, ...), custom_call_target="tpu_custom_call" | custom-call | tf_op jit(solution)/shard_map/add_up/pallas_call | solution.py:433
  433.8 2.2 unpack.1
  436.0 1.2 slice.46
  437.2 1.2 slice.51
  438.4 1.3 slice_bitcast_fusion.1
  439.7 1.6 copy.41
  441.3 1.6 copy.42
  (77 shorter events, 0.2 us)
Async XLA Ops:
  0.6 175.0 %copy-start = (bf16[256,256]{1,0:T(8,128)(2,1)S(1)}, bf16[256,256]{1,0:T(8,128)(2,1)}, u32[]{:S(2)}) copy-start(bf16[256,256]{1,0:T(8,128)(2,1)} %param.37) | copy-start | bytes 393220
  2.2 4.5 %copy-start.26 = (f32[2048]{0:T(1024)S(1)}, f32[2048]{0:T(1024)}, u32[]{:S(2)}) copy-start(f32[2048]{0:T(1024)} %param.28) | copy-start | bytes 24580
  13.6 2.9 copy-start.22
  13.6 2.9 copy-start.10
  13.6 3.8 copy-start.13
  13.6 3.8 copy-start.31
  19.1 56.6 %copy-start.30 = (s32[32,512]{1,0:T(8,128)S(1)}, s32[32,512]{1,0:T(8,128)}, u32[]{:S(2)}) copy-start(s32[32,512]{1,0:T(8,128)} %param.29) | copy-start | bytes 196612
  69.3 10.1 %all-to-all-start.5 = ((s32[32,1,640]{2,1,0:T(1,128)}), s32[32,1,640]{2,1,0:T(1,128)S(1)}, u32[]{:S(2)}, u32[]{:S(2)}) async-start(s32[32,1,640]{2,1,0:T(1,128)} %copy.38), calls=%async_computation.5 | async-start | bytes 163840 | tf_op jit(solution)/shard_map/all_to_all | solution.py:501
  118.3 1.0 copy-start.15
  118.3 1.0 copy-start.29
  118.3 0.9 copy-start.37
  119.2 3.8 copy-start.6
  123.1 48.7 %copy-start.20 = (bf16[256,256]{1,0:T(8,128)(2,1)S(1)}, bf16[256,256]{1,0:T(8,128)(2,1)}, u32[]{:S(2)}) copy-start(bf16[256,256]{1,0:T(8,128)(2,1)} %param.36) | copy-start | bytes 393220
  173.5 2.1 copy-start.16
  173.5 2.1 copy-start.36
  174.6 1.0 copy-start.11
  179.7 61.1 %copy-start.24 = (bf16[256,40]{0,1:T(8,128)(2,1)S(1)}, bf16[256,40]{0,1:T(8,128)(2,1)}, u32[]{:S(2)}) copy-start(bf16[256,40]{0,1:T(8,128)(2,1)} %param.39) | copy-start | bytes 61444
  241.9 0.9 copy-start.17
  241.9 0.9 copy-start.23
  241.9 0.9 copy-start.38
  242.8 2.4 copy-start.27
  242.8 2.4 copy-start.33
  242.8 3.2 copy-start.4
  246.0 2.5 copy-start.25
  312.2 2.6 copy-start.8
  314.9 1.6 copy-start.5
  314.9 1.6 copy-start.18
  316.5 1.6 copy-start.12
  318.0 1.7 copy-start.21
  381.4 2.2 copy-start.9
  383.6 1.2 copy-start.7
  383.6 1.2 copy-start.19
  384.8 1.4 copy-start.14
  384.8 2.4 copy-start.28
  384.8 2.4 copy-start.32
  384.8 3.7 copy-start.34
  384.8 3.7 copy-start.35

commit v4 on v3

--- a/solution.py
+++ b/solution.py
@@ -11,7 +11,7 @@
 LANES = 128
 DST_TILE = 256
 WINDOW = 8
-COLS = 512
+COLS = 1024
 BATCH = 8
 PLANE = 8
 ROWS = 512
@@ -34,7 +34,7 @@
     dst_iota = lax.broadcasted_iota(jnp.int32, (DST_TILE, LANES), 0) + tile * DST_TILE
     lanes = lax.broadcasted_iota(jnp.int32, (WINDOW * LANES, LANES), 1).astype(IDX)
 
-    def window_step(w, carry):
+    def window_step(w, add):
         rows = first + w * WINDOW
         dst = dst_ref[pl.ds(rows, WINDOW), :]
         col = col_ref[pl.ds(rows, WINDOW), :]
@@ -45,31 +45,30 @@
 
         def fill(out_ref, base):
             def block_step(b, carry):
-                offset = pl.multiple_of(b * COLS, COLS)
+                offset = b * COLS
                 shifted = columns - (base + offset).astype(IDX)
-                hot = jnp.concatenate([jnp.where(shifted == lanes + IDX(j * LANES), BF16(1), BF16(0))
-                                       for j in range(COLS // LANES)], axis=1)
-                counts = jnp.dot(to_dst, hot, preferred_element_type=F32)
-                at = (slice(None), pl.ds(offset, COLS))
-
-                @pl.when(w == 0)
-                def _():
+                for c in range(0, COLS, 2 * LANES):
+                    hot = jnp.concatenate([jnp.where(shifted == lanes + IDX(c + j * LANES), BF16(1), BF16(0))
+                                           for j in range(2)], axis=1)
+                    counts = jnp.dot(to_dst, hot, preferred_element_type=F32)
+                    at = (slice(None), pl.ds(pl.multiple_of(offset + c, 2 * LANES), 2 * LANES))
+                    if add:
+                        counts = counts + out_ref[at].astype(F32)
                     out_ref[at] = counts.astype(BF16)
-
-                @pl.when(w > 0)
-                def _():
-                    out_ref[at] = (out_ref[at].astype(F32) + counts).astype(BF16)
-
                 return carry
 
             lax.fori_loop(0, out_ref.shape[1] // COLS, block_step, 0)
 
         fill(own_ref, 0)
         fill(rec_ref, n_own)
+
+    window_step(0, False)
+
+    def more(w, carry):
+        window_step(w, True)
         return carry
 
-    windows = jnp.maximum(lax.div(last - first + WINDOW - 1, WINDOW), 1)
-    lax.fori_loop(0, windows, window_step, 0)
+    lax.fori_loop(1, lax.div(last - first + WINDOW - 1, WINDOW), more, 0)
 
 
 def adjacency(part, starts, dst_idx, columns, n_own, n_recv):
@@ -182,10 +181,10 @@
     n_own, n_recv = adj_rec.shape
     width = rows.shape[1]
     return pl.pallas_call(
-        spread_out_kernel, grid=(n_recv // COLS,),
-        in_specs=[pl.BlockSpec((n_own, COLS), lambda i: (0, i)),
+        spread_out_kernel, grid=(n_recv // 512,),
+        in_specs=[pl.BlockSpec((n_own, 512), lambda i: (0, i)),
                   pl.BlockSpec((n_own, width), lambda i: (0, 0))],
-        out_specs=pl.BlockSpec((COLS, width), lambda i: (i, 0)),
+        out_specs=pl.BlockSpec((512, width), lambda i: (i, 0)),
         out_shape=jax.ShapeDtypeStruct((n_recv, width), BF16),
         compiler_params=pltpu.CompilerParams(vmem_limit_bytes=VMEM_BYTES),
         cost_estimate=pl.CostEstimate(flops=2 * n_own * n_recv * width, bytes_accessed=20 * 10**6, transcendentals=0),
@@ -193,11 +192,13 @@
     )(adj_rec, rows)
 
 
-def plane_order(me, planes):
+def plane_order(me):
     z = lax.div(me, PLANE)
-    if planes == 4:
-        return [lax.rem(z + 2, 4), 3 - z, z + 1 - 2 * lax.rem(z, 2), z]
-    return [lax.rem(z + step, planes) for step in range(1, planes + 1)]
+    near, far, mirror = z + 1 - 2 * lax.rem(z, 2), lax.rem(z + 2, 4), 3 - z
+    inner = lax.div(lax.rem(z, 3) + 1, 2)
+    sending = [inner * far + (1 - inner) * near, inner * mirror + (1 - inner) * far,
+               inner * near + (1 - inner) * mirror, z]
+    return sending, [z, near, far, mirror]
 
 
 def meet_all(barrier, me, group):
@@ -251,11 +252,11 @@
 def exchange_in_kernel(group, list_ref, rows_ref, own_hbm, rec_hbm, out_ref,
                        outbox, inbox, own_ref, rec_ref, send, recv, sems):
     me = lax.axis_index(GROUP_AXIS)
-    planes = plane_order(me, group // PLANE)
+    planes, arriving = plane_order(me)
     barrier = pltpu.get_barrier_semaphore()
     meet_all(barrier, me, group)
-    own_copy, rec_copies = fetch_adjacency(own_hbm, rec_hbm, own_ref, rec_ref, planes, sems)
-    for item in [own_copy] + rec_copies[::-1]:
+    own_copy, rec_copies = fetch_adjacency(own_hbm, rec_hbm, own_ref, rec_ref, arriving, sems)
+    for item in [own_copy] + rec_copies:
         item.start()
     swap = Swap(me, outbox, inbox, send, recv)
     n_rows = rows_ref.shape[0]
@@ -283,9 +284,9 @@
         return carry
 
     lax.fori_loop(0, n_rows // ROWS, own_step, 0)
-    for k in [3, 2, 0, 1] if len(planes) == 4 else range(len(planes))[::-1]:
+    for k, plane in enumerate(arriving):
         rec_copies[k].wait()
-        block = swap.receive_plane(planes[k], k == len(planes) - 1)
+        block = swap.receive_plane(plane, k == 0)
 
         def rec_step(i, carry):
             at = pl.ds(pl.multiple_of(i * ROWS, ROWS), ROWS)
@@ -299,7 +300,7 @@
 def exchange_back_kernel(group, list_ref, grad_ref, add_ref, own_hbm, rec_hbm, out_ref,
                          outbox, inbox, own_ref, rec_ref, send, recv, sems):
     me = lax.axis_index(GROUP_AXIS)
-    planes = plane_order(me, group // PLANE)
+    planes, arriving = plane_order(me)
     barrier = pltpu.get_barrier_semaphore()
     meet_all(barrier, me, group)
     own_copy, rec_copies = fetch_adjacency(own_hbm, rec_hbm, own_ref, rec_ref, planes, sems)
@@ -326,9 +327,9 @@
 
     lax.fori_loop(0, n_rows // ROWS, own_step, 0)
     row_iota = lax.broadcasted_iota(jnp.int32, (ROWS, LANES), 0)
-    for k in [3, 2, 0, 1] if len(planes) == 4 else range(len(planes))[::-1]:
-        block = swap.receive_plane(planes[k], k == len(planes) - 1)
-        names = list_ref[pl.ds(pl.multiple_of(planes[k] * PLANE, PLANE), PLANE), :]
+    for k, plane in enumerate(arriving):
+        block = swap.receive_plane(plane, k == 0)
+        names = list_ref[pl.ds(pl.multiple_of(plane * PLANE, PLANE), PLANE), :]
 
         def rec_step(i, carry):
             at = pl.ds(pl.multiple_of(i * ROWS, ROWS), ROWS)

time: 451 us -> 429 us (0.951)
  the two profiles are of different devices: /device:TPU:29 before, /device:TPU:21 now
where the time goes in v4:
time: 429 us; the launch traced here: 421 us
  Pallas kernels  336 us (78%)
  matrix products  33.2 us (8%)
  other arithmetic  17.1 us (4%)
  local copies, waits for them, and re-layouts  12.7 us (3%)
  starting transfers between devices  6.75 us (2%)
  between operations  5.96 us (1%)
  loops' own time  4.7 us (1%)
  waiting for transfers between devices  4.29 us (1%)
    pallas_call x5, Pallas kernels, exchange(): pl.pallas_call(functools.partial(body, group), in_specs=[vmem] * (1 + len...  255 us
    pallas_call x1, Pallas kernels, adjacency(): pl.pallas_call(functools.partial(adjacency_kernel, n_own), grid_spec=grid...  40.9 us
    pallas_call x1, Pallas kernels, add_up(): pl.pallas_call(functools.partial(add_up_kernel, n_chips, rows), in_specs=...  38.4 us
    dot_general x3, matrix products, layer(): jnp.dot(neigh_mean, w_neigh, preferred_element_type=jnp.float32)  10.1 us
  transfers between devices with their start and end apart: 1, of which 1 were waited for; matrix products, arithmetic and copies ran while one was open for 0% of the time, Pallas kernels for 0%

profile of v4, /device:TPU:21, one launch (start us, length us, event | category | flops | bytes accessed | tf_op | source)
XLA Modules:
  0.0 421.0 jit_solution(3377470211851296913)
XLA Ops:
  0.6 0.0 copy-start
  0.7 0.8 add_compare_fusion.1
  1.4 0.8 add_select_fusion.3
  2.2 0.0 copy-start.26
  2.2 2.3 fusion.10
  4.6 0.9 fusion.25
  6.7 0.6 reduce_sum.100
  9.4 0.7 copy.38
  10.1 3.5 fusion.16
  13.6 0.0 copy-start.22
  13.6 2.9 fusion.1
  16.5 0.2 convert_reduce_fusion.starts
  16.7 0.6 pad_bitcast_fusion.10
  17.4 1.8 fusion.44
  19.1 40.9 %adjacency.6 = (bf16[2048,2048]{1,0:T(8,128)(2,1)}, bf16[2048,4096]{1,0:T(8,128)(2,1)}) custom-call(s32[9]{0:T(128)S(1)} %convert_reduce_fusion.starts, s32[1]{0:T(128)} %constant.134.clone.1.parts, s32[56,128]{1,0:T(8,128)} %get-tuple-element.405.dst_ref, s32[56,128]{1,0:T(8,128)} %get-tuple-element.404.col_ref), custom_call_target="tpu_custom_call" | custom-call | flops 30000001024 | bytes 40000000 | tf_op jit(solution)/shard_map/adjacency/pallas_call | solution.py:85
  60.1 6.8 %all-to-all-start.5 = ((s32[32,1,640]{2,1,0:T(1,128)}), s32[32,1,640]{2,1,0:T(1,128)S(1)}, u32[]{:S(2)}, u32[]{:S(2)}) async-start(s32[32,1,640]{2,1,0:T(1,128)} %copy.38), calls=%async_computation.5 | async-start | bytes 163840 | tf_op jit(solution)/shard_map/all_to_all | solution.py:502
  66.9 4.3 %all-to-all-done.5 = s32[32,1,640]{2,1,0:T(1,128)S(1)} async-done(((s32[32,1,640]{2,1,0:T(1,128)}), s32[32,1,640]{2,1,0:T(1,128)S(1)}, u32[]{:S(2)}, u32[]{:S(2)}) %all-to-all-start.5) | async-done | bytes 81952 | tf_op jit(solution)/shard_map/all_to_all | solution.py:502
  71.2 0.7 slice_reduce_fusion.1
  72.5 4.2 select_reduce_fusion
  76.7 0.6 slice_bitcast_fusion.list_ref
  77.3 30.2 %exchange_in.3 = f32[2048,128]{1,0:T(8,128)S(1)} custom-call(s32[32,128]{1,0:T(8,128)} %slice_bitcast_fusion.list_ref, bf16[2048,128]{1,0:T(8,128)(2,1)S(1)} %copy-done.13, bf16[2048,2048]{1,0:T(8,128)(2,1)} %get-tuple-element.239.own_hbm, bf16[2048,4096]{1,0:T(8,128)(2,1)} %get-tuple-element.240.rec_hbm), custom_call_target="tpu_custom_call" | custom-call | flops 4294967296 | bytes 30000000 | tf_op jit(solution)/shard_map/exchange_in/pallas_call | solution.py:353
  107.5 0.9 while.50
  108.4 3.8 maximum_convert_fusion.1
  112.2 56.1 %exchange_in.4 = f32[2048,256]{1,0:T(8,128)} custom-call(s32[32,128]{1,0:T(8,128)} %slice_bitcast_fusion.list_ref, bf16[2048,256]{1,0:T(8,128)(2,1)S(1)} %get-tuple-element.726.rows_ref, bf16[2048,2048]{1,0:T(8,128)(2,1)} %get-tuple-element.239.own_hbm, bf16[2048,4096]{1,0:T(8,128)(2,1)} %get-tuple-element.240.rec_hbm), custom_call_target="tpu_custom_call" | custom-call | flops 8589934592 | bytes 30000000 | tf_op jit(solution)/shard_map/exchange_in/pallas_call | solution.py:353
  168.4 1.7 fusion.45
  170.1 1.1 while.51
  171.2 1.0 copy-done.11
  172.2 4.1 maximum_convert_fusion
  176.3 55.8 %exchange_in.5 = f32[2048,256]{1,0:T(8,128)} custom-call(s32[32,128]{1,0:T(8,128)} %slice_bitcast_fusion.list_ref, bf16[2048,256]{1,0:T(8,128)(2,1)S(1)} %get-tuple-element.759.rows_ref, bf16[2048,2048]{1,0:T(8,128)(2,1)} %get-tuple-element.239.own_hbm, bf16[2048,4096]{1,0:T(8,128)(2,1)} %get-tuple-element.240.rec_hbm), custom_call_target="tpu_custom_call" | custom-call | flops 8589934592 | bytes 30000000 | tf_op jit(solution)/shard_map/exchange_in/pallas_call | solution.py:353
  232.1 1.2 fusion.46
  233.3 0.9 while.52
  234.2 2.3 fusion.43
  236.5 0.1 exponential_reduce_fusion
  236.6 0.8 select_reduce_fusion.1
  237.3 1.1 fusion.42.refs_5_
  238.4 0.9 fusion.50.refs_4_
  239.3 0.5 fusion.8.grad_ref
  239.9 1.8 fusion.47.add_ref
  241.6 55.9 %exchange_back.2 = f32[2048,256]{1,0:T(8,128)S(1)} custom-call(s32[32,128]{1,0:T(8,128)} %slice_bitcast_fusion.list_ref, bf16[2048,256]{1,0:T(8,128)(2,1)S(1)} %fusion.8.grad_ref, f32[2048,256]{1,0:T(8,128)} %fusion.47.add_ref, bf16[2048,2048]{1,0:T(8,128)(2,1)} %get-tuple-element.239.own_hbm, bf16[2048,4096]{1,0:T(8,128)(2,1)} %get-tuple-element.240.rec_hbm), custom_call_target="tpu_custom_call" | custom-call | flops 8589934592 | bytes 30000000 | tf_op jit(solution)/shard_map/exchange_back/pallas_call | solution.py:353
  297.6 1.1 while.53
  298.6 2.6 fusion.13
  301.2 0.4 fusion.14
  301.7 1.2 copy-done.5
  302.8 1.6 fusion.41.refs_3_
  304.4 1.2 fusion.49.refs_2_
  305.6 0.5 fusion.7.grad_ref
  306.1 1.8 fusion.48.add_ref
  307.9 56.8 %exchange_back.3 = f32[2048,256]{1,0:T(8,128)S(1)} custom-call(s32[32,128]{1,0:T(8,128)} %slice_bitcast_fusion.list_ref, bf16[2048,256]{1,0:T(8,128)(2,1)S(1)} %fusion.7.grad_ref, f32[2048,256]{1,0:T(8,128)} %fusion.48.add_ref, bf16[2048,2048]{1,0:T(8,128)(2,1)} %get-tuple-element.239.own_hbm, bf16[2048,4096]{1,0:T(8,128)(2,1)} %get-tuple-element.240.rec_hbm), custom_call_target="tpu_custom_call" | custom-call | flops 8589934592 | bytes 30000000 | tf_op jit(solution)/shard_map/exchange_back/pallas_call | solution.py:353
  364.7 0.8 while.54
  365.6 2.1 fusion.11
  367.6 0.2 copy-done.9
  367.8 0.4 fusion.12
  368.2 0.8 copy-done.7
  369.0 1.4 fusion.40.refs_1_
  370.4 1.0 convolution_bitcast_fusion.refs_0_
  371.4 0.6 multiply_reduce_fusion
  372.7 0.6 pad.21.refs_6_
  373.3 38.4 %add_up.1.packed_ref = f32[1792,128]{1,0:T(8,128)} custom-call(f32[128,256]{1,0:T(8,128)} %convolution_bitcast_fusion.refs_0_, f32[128,256]{1,0:T(8,128)} %fusion.40.refs_1_, f32[256,256]{1,0:T(8,128)} %fusion.49.refs_2_, f32[256,256]{1,0:T(8,128)} %fusion.41.refs_3_, f32[40,256]{1,0:T(8,128)} %fusion.50.refs_4_, f32[40,256]{1,0:T(8,128)} %fusion.42.refs_5_, ...), custom_call_target="tpu_custom_call" | custom-call | tf_op jit(solution)/shard_map/add_up/pallas_call | solution.py:434
  411.7 2.2 unpack.1
  413.9 1.2 slice.46
  415.1 1.2 slice.51
  416.3 1.3 slice_bitcast_fusion.1
  417.6 1.6 copy.41
  419.2 1.6 copy.42
  (77 shorter events, 0.2 us)
Async XLA Ops:
  0.6 171.5 %copy-start = (bf16[256,256]{1,0:T(8,128)(2,1)S(1)}, bf16[256,256]{1,0:T(8,128)(2,1)}, u32[]{:S(2)}) copy-start(bf16[256,256]{1,0:T(8,128)(2,1)} %param.37) | copy-start | bytes 393220
  2.2 4.5 %copy-start.26 = (f32[2048]{0:T(1024)S(1)}, f32[2048]{0:T(1024)}, u32[]{:S(2)}) copy-start(f32[2048]{0:T(1024)} %param.28) | copy-start | bytes 24580
  13.6 2.9 copy-start.22
  13.6 2.9 copy-start.10
  13.6 3.8 copy-start.13
  13.6 3.8 copy-start.31
  19.1 47.7 %copy-start.30 = (s32[32,512]{1,0:T(8,128)S(1)}, s32[32,512]{1,0:T(8,128)}, u32[]{:S(2)}) copy-start(s32[32,512]{1,0:T(8,128)} %param.29) | copy-start | bytes 196612
  60.1 11.1 %all-to-all-start.5 = ((s32[32,1,640]{2,1,0:T(1,128)}), s32[32,1,640]{2,1,0:T(1,128)S(1)}, u32[]{:S(2)}, u32[]{:S(2)}) async-start(s32[32,1,640]{2,1,0:T(1,128)} %copy.38), calls=%async_computation.5 | async-start | bytes 163840 | tf_op jit(solution)/shard_map/all_to_all | solution.py:502
  107.5 0.9 copy-start.15
  107.5 0.9 copy-start.29
  107.5 0.9 copy-start.37
  108.4 3.8 copy-start.6
  112.2 56.1 %copy-start.20 = (bf16[256,256]{1,0:T(8,128)(2,1)S(1)}, bf16[256,256]{1,0:T(8,128)(2,1)}, u32[]{:S(2)}) copy-start(bf16[256,256]{1,0:T(8,128)(2,1)} %param.36) | copy-start | bytes 393220
  170.1 2.1 copy-start.16
  170.1 2.1 copy-start.36
  171.2 1.0 copy-start.11
  176.3 55.8 %copy-start.24 = (bf16[256,40]{0,1:T(8,128)(2,1)S(1)}, bf16[256,40]{0,1:T(8,128)(2,1)}, u32[]{:S(2)}) copy-start(bf16[256,40]{0,1:T(8,128)(2,1)} %param.39) | copy-start | bytes 61444
  233.3 0.9 copy-start.17
  233.3 0.9 copy-start.23
  233.3 0.9 copy-start.38
  234.1 2.4 copy-start.27
  234.1 2.4 copy-start.33
  234.2 3.2 copy-start.4
  237.3 2.5 copy-start.25
  298.6 2.6 copy-start.8
  301.2 1.6 copy-start.5
  301.2 1.6 copy-start.18
  302.8 1.6 copy-start.12
  304.4 1.7 copy-start.21
  365.6 2.2 copy-start.9
  367.8 1.2 copy-start.7
  367.8 1.2 copy-start.19
  369.0 1.4 copy-start.14
  369.0 2.4 copy-start.28
  369.0 2.4 copy-start.32
  369.0 3.7 copy-start.34
  369.0 3.7 copy-start.35
